TPU v7x, 256 devices: a whole 4x4x8 slice. The times are simulated.
256 devices in a mesh: tm: 64 (over y, z, x_hi), space: 4 (over x_lo, core).
Axes of the slice: x: 4 (x_hi: 2, x_lo: 2; x = x_hi * 2 + x_lo), y: 4, z: 8, core: 2. Of those that a mesh axis runs over, the one named last changes fastest.
Arguments:
- initial: float32 [8, 128, 128], P('space'), may hold values from -6 to 6
- start_guess: float32 [64, 8, 128, 128], P('tm', 'space'), may hold values from -6 to 6
- forcing: float32 [64, 5, 8, 128, 128], P('tm', None, 'space'), may hold values from -6 to 6
- step_size: float32 [64], P('tm'), may hold values from 0.06 to 0.16
Outputs:
- fine_values: float32 [64, 5, 8, 128, 128], P('tm', None, 'space')
All inputs are finite; a program needn't handle non-finite values.
Results may differ from a plain program's by a relative error of at most 0.0001.
Values sent between devices are 32-bit elements; how exact they have to be, the bound alone decides.
A program may use at most 64 MiB of HBM per device.

v0:
```python
import math

import jax
import jax.numpy as jnp
import numpy as np
from jax import lax
from jax.sharding import Mesh
from jax.sharding import PartitionSpec as P

ITERS = 2
TM = ("tm_0", "tm_1", "tm_2")


def with_halo(block, sides, width):
    for axis, dim in sides:
        count = lax.axis_size(axis)
        forward = [(i, i + 1) for i in range(count - 1)]
        backward = [(target, source) for source, target in forward]
        low = lax.ppermute(
            lax.slice_in_dim(block, block.shape[dim] - width, None, axis=dim), axis, forward
        )
        high = lax.ppermute(lax.slice_in_dim(block, 0, width, axis=dim), axis, backward)
        block = jnp.concatenate([low, block, high], axis=dim)
    return block


def copy_for_each(x, axis):
    devices = lax.axis_size(axis)
    return lax.all_to_all(jnp.broadcast_to(x[None], (devices, *x.shape)), axis, 0, 0, tiled=True)


def in_order(tiles, dim):
    shape = list(tiles.shape[1:])
    shape[dim] *= tiles.shape[0]
    return jnp.moveaxis(tiles, 0, dim).reshape(shape)


def gather_directly(x, axis, dim):
    tiles = copy_for_each(x, axis)
    return in_order(tiles, dim)


def shifted(value, axis, steps):
    count = lax.axis_size(axis)
    first, last = (max(0, -steps), min(count, count - steps))
    return lax.ppermute(value, axis, [(source, source + steps) for source in range(first, last)])


def nothing_yet(x, identity):
    return jax.tree.map(
        lambda part, zero: jnp.zeros_like(part) + jnp.asarray(zero, part.dtype), x, identity
    )


def carried_in(x, axes, combine, identity):
    before = start = nothing_yet(x, identity)
    subtotal = x
    for axis in reversed(axes):
        devices, here = (lax.axis_size(axis), lax.axis_index(axis))
        pieces = jax.tree.map(lambda part: lax.all_gather(part, axis), subtotal)
        inside, subtotal = (start, start)
        for k in range(devices):
            passed = k < here
            subtotal = combine(subtotal, jax.tree.map(lambda part: part[k], pieces))
            inside = jax.tree.map(lambda new, old: jnp.where(passed, new, old), subtotal, inside)
        before = combine(inside, before)
    return before


def node_tables():
    radical = math.sqrt(3.0 / 7.0)
    node_times = [0.0, (1.0 - radical) / 2.0, 0.5, (1.0 + radical) / 2.0, 1.0]
    integrals = np.zeros((4, 5))
    for column in range(5):
        coeffs = [1.0]
        for other_index in range(5):
            if other_index == column:
                continue
            other_time = node_times[other_index]
            scaling = node_times[column] - other_time
            grown = [0.0] * (len(coeffs) + 1)
            for exponent in range(len(coeffs)):
                grown[exponent + 1] += coeffs[exponent] / scaling
                grown[exponent] -= coeffs[exponent] * other_time / scaling
            coeffs = grown
        for section in range(4):
            integrals[section, column] = sum(
                (
                    coeffs[exponent]
                    * (
                        node_times[section + 1] ** (exponent + 1)
                        - node_times[section] ** (exponent + 1)
                    )
                    / (exponent + 1)
                    for exponent in range(len(coeffs))
                )
            )
    coarse = [0.0, 0.5, 1.0]
    interp = np.zeros((5, 3))
    for column in range(3):
        for section in range(5):
            weight = 1.0
            for other_index in range(3):
                if other_index != column:
                    weight = (
                        weight
                        * (node_times[section] - coarse[other_index])
                        / (coarse[column] - coarse[other_index])
                    )
            interp[section, column] = weight
    return (np.array(node_times), integrals, interp)


def stencil(padded):
    center = padded[..., 1:-1, :, :]
    widths = [(0, 0)] * (center.ndim - 2) + [(1, 1), (1, 1)]
    framed = jnp.pad(center, widths)
    return (
        padded[..., 2:, :, :]
        + padded[..., :-2, :, :]
        + framed[..., 2:, 1:-1]
        + framed[..., :-2, 1:-1]
        + framed[..., 1:-1, 2:]
        + framed[..., 1:-1, :-2]
        - 6.0 * center
    )


def laplace_one(field):
    return stencil(with_halo(field, (("space", 0),), 1))


def laplace_nodes(fields):
    return stencil(with_halo(fields, (("space", 1),), 1))


def sine_matrix(length, row_first, row_count, col_count):
    rows = jnp.arange(row_count, dtype=jnp.int32) + row_first + 1
    columns = jnp.arange(col_count, dtype=jnp.int32) + 1
    phase = rows[:, None] * columns[None, :] % (2 * (length + 1))
    return math.sqrt(2.0 / (length + 1)) * jnp.sin(
        math.pi / (length + 1) * phase.astype(jnp.float32)
    )


def eigen_weights(length, first, count):
    indices = (jnp.arange(count, dtype=jnp.int32) + first + 1).astype(jnp.float32)
    return 2.0 - 2.0 * jnp.cos(math.pi / (length + 1) * indices)


def compose(earlier, later):
    return (earlier[0] * later[0], later[0] * earlier[1] + later[1])


def body(initial, start_guess, forcing, step_size):
    depth, width_x, width_y = initial.shape
    length_z = depth * lax.axis_size("space")
    z_first = lax.axis_index("space") * depth
    position = lax.axis_index(TM)
    highest = lax.Precision.HIGHEST
    x_matrix = sine_matrix(width_x, 0, width_x, width_x)
    y_matrix = sine_matrix(width_y, 0, width_y, width_y)
    eigen = (
        eigen_weights(length_z, z_first, depth)[:, None, None]
        + eigen_weights(width_x, 0, width_x)[None, :, None]
        + eigen_weights(width_y, 0, width_y)[None, None, :]
    )

    def lateral(field):
        mixed = jnp.einsum("ai,zij->zaj", x_matrix, field, precision=highest)
        return jnp.einsum("zaj,bj->zab", mixed, y_matrix, precision=highest)

    def forward(field):
        flat = lateral(field).reshape(depth, width_x * width_y)
        shard_rows = gather_directly(flat, "space", 0)
        spectral = jnp.zeros_like(flat) + jnp.dot(
            sine_matrix(length_z, z_first, depth, shard_rows.shape[0]),
            shard_rows,
            precision=highest,
            preferred_element_type=jnp.float32,
        )
        return spectral.reshape(depth, width_x, width_y)

    node_times, integrals, interp = node_tables()
    full_step = step_size[0]
    half_step = 0.5 * full_step
    initial_hat = forward(initial)
    values = jnp.broadcast_to(start_guess[0][None], (5, depth, width_x, width_y))
    for sweep_round in range(ITERS):
        previous = shifted(values[4], TM, 1)
        values = values.at[0].set(jnp.where(position == 0, initial, previous))
        lap_old = laplace_nodes(values)
        rates = lap_old + forcing[0]
        swept = [values[0]]
        lap_new = [lap_old[0]]
        for section in range(4):
            quadrature = sum(
                (float(integrals[section, column]) * rates[column] for column in range(5))
            )
            spacing = float(node_times[section + 1] - node_times[section])
            advanced = (
                swept[section]
                + full_step * spacing * (lap_new[section] - lap_old[section])
                + full_step * quadrature
            )
            swept.append(advanced)
            lap_new.append(laplace_one(advanced))
        new_rates = [lap_new[column] + forcing[0, column] for column in range(5)]
        first_half = full_step * sum(
            (
                float(integrals[0, column] + integrals[1, column]) * new_rates[column]
                for column in range(5)
            )
        )
        second_half = full_step * sum(
            (
                float(integrals[2, column] + integrals[3, column]) * new_rates[column]
                for column in range(5)
            )
        )
        left = first_half - half_step * lap_new[0]
        right = second_half - half_step * lap_new[2]
        forced = left + half_step * laplace_one(left) + right
        forced_hat = forward(forced)
        factor = 1.0 - half_step * eigen
        prefix_gain, prefix_sum = carried_in(
            (factor * factor, forced_hat),
            TM,
            compose,
            (jnp.ones_like(eigen), jnp.zeros_like(eigen)),
        )
        inverse_flat = (prefix_gain * initial_hat + prefix_sum).reshape(depth, width_x * width_y)
        accumulate_shard_rows = lax.all_gather(inverse_flat, "space", axis=0, tiled=True)
        physical = jnp.zeros_like(inverse_flat) + jnp.dot(
            sine_matrix(length_z, z_first, depth, accumulate_shard_rows.shape[0]),
            accumulate_shard_rows,
            precision=highest,
            preferred_element_type=jnp.float32,
        )
        coarse_first = lateral(physical.reshape(depth, width_x, width_y))
        coarse_middle = coarse_first + half_step * laplace_one(coarse_first) + left
        coarse_ending = coarse_middle + half_step * laplace_one(coarse_middle) + right
        deltas = [coarse_first - swept[0], coarse_middle - swept[2], coarse_ending - swept[4]]
        values = jnp.stack(
            [
                swept[section]
                + sum((float(interp[section, column]) * deltas[column] for column in range(3)))
                for section in range(5)
            ]
        )
    return values[None]


def solution(mesh):
    split = Mesh(
        mesh.devices.reshape(4, 8, 2, mesh.shape["space"]), ("tm_0", "tm_1", "tm_2", "space")
    )
    placed = (
        P("space", None, None),
        P(TM, "space", None, None),
        P(TM, None, "space", None, None),
        P(TM),
    )
    return jax.shard_map(
        body,
        mesh=split,
        in_specs=placed,
        out_specs=P(TM, None, "space", None, None),
        check_vma=False,
    )
```

profile of v0, /device:TPU:1, one launch (start us, length us, event | category | flops | bytes accessed | tf_op | source)
XLA Modules:
  0.0 381.7 jit_solution(3461902579520612439)
XLA Ops:
  6.5 5.5 %collective-permute-start = (f32[2,128,128]{2,1,0:T(8,128)}, f32[2,128,128]{2,1,0:T(8,128)S(1)}, u32[]{:S(2)}, u32[]{:S(2)}) collective-permute-start(f32[2,128,128]{2,1,0:T(8,128)} %bitcast.636), channel_id=1, source_target_pairs={{0,4},{4,8},{8,12},{12,16},{16,20},{20,24},{24,28},{28,32},{32,36}... | collective-permute-start | bytes 393224 | tf_op jit(solution)/shard_map/ppermute | solution.py:46
  29.5 4.5 %collective-permute-start.4 = (f32[1,128,128]{2,1,0:T(8,128)S(1)}, f32[1,128,128]{2,1,0:T(8,128)S(1)}, u32[]{:S(2)}, u32[]{:S(2)}) collective-permute-start(f32[1,128,128]{2,1,0:T(8,128)S(1)} %get-tuple-element.96), channel_id=1, source_target_pairs={{0,1},{1,2},{2,3},{4,5},{5,6},{6,7},{8,9},{9,10},{10,11},{12,13},{... | collective-permute-start | bytes 196616 | tf_op jit(solution)/shard_map/ppermute | solution.py:19
  37.4 4.3 %collective-permute-start.6 = (f32[1,128,128]{2,1,0:T(8,128)S(1)}, f32[1,128,128]{2,1,0:T(8,128)S(1)}, u32[]{:S(2)}, u32[]{:S(2)}) collective-permute-start(f32[1,128,128]{2,1,0:T(8,128)S(1)} %get-tuple-element.94), channel_id=1, source_target_pairs={{0,1},{1,2},{2,3},{4,5},{5,6},{6,7},{8,9},{9,10},{10,11},{12,13},{... | collective-permute-start | bytes 196616 | tf_op jit(solution)/shard_map/ppermute | solution.py:19
  60.5 4.3 %collective-permute-start.12 = (f32[1,128,128]{2,1,0:T(8,128)S(1)}, f32[1,128,128]{2,1,0:T(8,128)S(1)}, u32[]{:S(2)}, u32[]{:S(2)}) collective-permute-start(f32[1,128,128]{2,1,0:T(8,128)S(1)} %get-tuple-element.88), channel_id=1, source_target_pairs={{0,1},{1,2},{2,3},{4,5},{5,6},{6,7},{8,9},{9,10},{10,11},{12,13},{... | collective-permute-start | bytes 196616 | tf_op jit(solution)/shard_map/ppermute | solution.py:19
  72.6 13.0 %all_gather.22 = f32[2,2,128,128]{3,2,1,0:T(8,128)S(1)} all-gather(f32[1,2,128,128]{3,2,1,0:T(8,128)S(1)} %subtract_multiply_fusion), channel_id=1, replica_groups=mesh['tm_0'=4,'tm_1'=8,'tm_2'=2,'space'=4] {'tm_2'}, dimensions={0}, use_global_device_ids=true | all-gather | bytes 393216 | tf_op jit(solution)/shard_map/all_gather | solution.py:60
  86.6 6.6 %all-gather = f32[4,128,128]{2,1,0:T(8,128)S(1)} all-gather(f32[2,128,128]{2,1,0:T(8,128)S(1)} %copy.110), channel_id=2, replica_groups=mesh['tm_0'=4,'tm_1'=8,'tm_2'=2,'space'=4] {'tm_2'}, dimensions={0}, use_global_device_ids=true | all-gather | bytes 393216 | tf_op jit(solution)/shard_map/all_gather | solution.py:60
  97.0 4.9 %all-to-all-start = ((f32[4,2,16384]{2,1,0:T(2,128)}), f32[4,2,16384]{2,1,0:T(2,128)S(1)}, u32[]{:S(2)}, u32[]{:S(2)}) async-start(f32[4,2,16384]{2,1,0:T(2,128)} %broadcast_in_dim.21), calls=%async_computation | async-start | bytes 1048576 | tf_op jit(solution)/shard_map/all_to_all | solution.py:29
  101.9 7.8 %all-to-all-done = f32[4,2,16384]{2,1,0:T(2,128)S(1)} async-done(((f32[4,2,16384]{2,1,0:T(2,128)}), f32[4,2,16384]{2,1,0:T(2,128)S(1)}, u32[]{:S(2)}, u32[]{:S(2)}) %all-to-all-start) | async-done | bytes 524320 | tf_op jit(solution)/shard_map/all_to_all | solution.py:29
  110.8 20.8 %all-gather.8.cloned.1.call-done = f32[8,2,128,128]{3,2,1,0:T(8,128)} async-done(((f32[1,2,128,128]{3,2,1,0:T(8,128)}), f32[8,2,128,128]{3,2,1,0:T(8,128)}) %all-gather.8.cloned.1.call-update) | async-done | bytes 1048592 | tf_op jit(solution)/shard_map/all_gather | solution.py:60
  133.0 10.2 %all_gather.48 = f32[4,2,128,128]{3,2,1,0:T(8,128)S(1)} all-gather(f32[1,2,128,128]{3,2,1,0:T(8,128)S(1)} %multiply_multiply_fusion), channel_id=1, replica_groups=mesh['tm_0'=4,'tm_1'=8,'tm_2'=2,'space'=4] {'tm_0'}, dimensions={0}, use_global_device_ids=true | all-gather | bytes 655360 | tf_op jit(solution)/shard_map/all_gather | solution.py:60
  143.3 27.0 %all-gather.10.cloned.1.call-done = f32[8,2,128,128]{3,2,1,0:T(8,128)} async-done(((f32[1,2,128,128]{3,2,1,0:T(8,128)}), f32[8,2,128,128]{3,2,1,0:T(8,128)}) %all-gather.10.cloned.1.call-update) | async-done | bytes 1048592 | tf_op jit(solution)/shard_map/all_gather | solution.py:60
  171.7 10.2 %all_gather.51 = f32[4,2,128,128]{3,2,1,0:T(8,128)S(1)} all-gather(f32[1,2,128,128]{3,2,1,0:T(8,128)S(1)} %multiply_add_fusion.1), channel_id=1, replica_groups=mesh['tm_0'=4,'tm_1'=8,'tm_2'=2,'space'=4] {'tm_0'}, dimensions={0}, use_global_device_ids=true | all-gather | bytes 655360 | tf_op jit(solution)/shard_map/all_gather | solution.py:60
  183.1 15.8 %all-gather.2 = f32[4,2,16384]{2,1,0:T(2,128)S(1)} all-gather(f32[1,2,16384]{2,1,0:T(2,128)} %reshape.443), channel_id=1, replica_groups=mesh['tm_0'=4,'tm_1'=8,'tm_2'=2,'space'=4] {'space'}, dimensions={0}, use_global_device_ids=true | all-gather | bytes 655360 | tf_op jit(solution)/shard_map/all_gather | solution.py:233
  212.0 4.4 %collective-permute-start.16 = (f32[1,128,128]{2,1,0:T(8,128)S(1)}, f32[1,128,128]{2,1,0:T(8,128)S(1)}, u32[]{:S(2)}, u32[]{:S(2)}) collective-permute-start(f32[1,128,128]{2,1,0:T(8,128)S(1)} %get-tuple-element.84), channel_id=1, source_target_pairs={{0,1},{1,2},{2,3},{4,5},{5,6},{6,7},{8,9},{9,10},{10,11},{12,13},{... | collective-permute-start | bytes 196616 | tf_op jit(solution)/shard_map/ppermute | solution.py:19
  218.0 4.5 %collective-permute-start.17 = (f32[2,128,128]{2,1,0:T(8,128)S(1)}, f32[2,128,128]{2,1,0:T(8,128)S(1)}, u32[]{:S(2)}, u32[]{:S(2)}) collective-permute-start(f32[2,128,128]{2,1,0:T(8,128)S(1)} %get-tuple-element.46), channel_id=1, source_target_pairs={{0,4},{4,8},{8,12},{12,16},{16,20},{20,24},{24,28},{28,32},{32,36}... | collective-permute-start | bytes 393224 | tf_op jit(solution)/shard_map/ppermute | solution.py:46
  226.3 4.5 %collective-permute-start.19 = (f32[5,1,128,128]{3,2,1,0:T(8,128)S(1)}, f32[5,1,128,128]{3,2,1,0:T(8,128)S(1)}, u32[]{:S(2)}, u32[]{:S(2)}) collective-permute-start(f32[5,1,128,128]{3,2,1,0:T(8,128)S(1)} %get-tuple-element.64), channel_id=1, source_target_pairs={{0,1},{1,2},{2,3},{4,5},{5,6},{6,7},{8,9},{9,10},{10,11},{12,13},{... | collective-permute-start | bytes 983048 | tf_op jit(solution)/shard_map/ppermute | solution.py:19
  237.3 4.4 %collective-permute-start.21 = (f32[1,128,128]{2,1,0:T(8,128)S(1)}, f32[1,128,128]{2,1,0:T(8,128)S(1)}, u32[]{:S(2)}, u32[]{:S(2)}) collective-permute-start(f32[1,128,128]{2,1,0:T(8,128)S(1)} %get-tuple-element.82), channel_id=1, source_target_pairs={{0,1},{1,2},{2,3},{4,5},{5,6},{6,7},{8,9},{9,10},{10,11},{12,13},{... | collective-permute-start | bytes 196616 | tf_op jit(solution)/shard_map/ppermute | solution.py:19
  245.1 4.3 %collective-permute-start.23 = (f32[1,128,128]{2,1,0:T(8,128)S(1)}, f32[1,128,128]{2,1,0:T(8,128)S(1)}, u32[]{:S(2)}, u32[]{:S(2)}) collective-permute-start(f32[1,128,128]{2,1,0:T(8,128)S(1)} %get-tuple-element.80), channel_id=1, source_target_pairs={{0,1},{1,2},{2,3},{4,5},{5,6},{6,7},{8,9},{9,10},{10,11},{12,13},{... | collective-permute-start | bytes 196616 | tf_op jit(solution)/shard_map/ppermute | solution.py:19
  260.5 4.3 %collective-permute-start.27 = (f32[1,128,128]{2,1,0:T(8,128)S(1)}, f32[1,128,128]{2,1,0:T(8,128)S(1)}, u32[]{:S(2)}, u32[]{:S(2)}) collective-permute-start(f32[1,128,128]{2,1,0:T(8,128)S(1)} %get-tuple-element.76), channel_id=1, source_target_pairs={{0,1},{1,2},{2,3},{4,5},{5,6},{6,7},{8,9},{9,10},{10,11},{12,13},{... | collective-permute-start | bytes 196616 | tf_op jit(solution)/shard_map/ppermute | solution.py:19
  275.4 11.6 %all_to_all.15 = f32[4,2,16384]{2,1,0:T(2,128)S(1)} all-to-all(f32[4,2,16384]{2,1,0:T(2,128)S(1)} %broadcast_in_dim.25), channel_id=1, replica_groups=mesh['tm_0'=4,'tm_1'=8,'tm_2'=2,'space'=4] {'space'}, dimensions={0} | all-to-all | bytes 1048576 | tf_op jit(solution)/shard_map/all_to_all | solution.py:29
  288.0 7.8 %all-gather.1 = f32[4,128,128]{2,1,0:T(8,128)S(1)} all-gather(f32[2,128,128]{2,1,0:T(8,128)S(1)} %copy.115), channel_id=3, replica_groups=mesh['tm_0'=4,'tm_1'=8,'tm_2'=2,'space'=4] {'tm_2'}, dimensions={0}, use_global_device_ids=true | all-gather | bytes 393216 | tf_op jit(solution)/shard_map/all_gather | solution.py:60
  296.5 32.9 %all-gather.12.cloned.1.call-done = f32[8,2,128,128]{3,2,1,0:T(8,128)} async-done(((f32[1,2,128,128]{3,2,1,0:T(8,128)}), f32[8,2,128,128]{3,2,1,0:T(8,128)}) %all-gather.12.cloned.1.call-update) | async-done | bytes 1048592 | tf_op jit(solution)/shard_map/all_gather | solution.py:60
  330.9 10.2 %all_gather.55 = f32[4,2,128,128]{3,2,1,0:T(8,128)S(1)} all-gather(f32[1,2,128,128]{3,2,1,0:T(8,128)S(1)} %multiply_add_fusion), channel_id=1, replica_groups=mesh['tm_0'=4,'tm_1'=8,'tm_2'=2,'space'=4] {'tm_0'}, dimensions={0}, use_global_device_ids=true | all-gather | bytes 655360 | tf_op jit(solution)/shard_map/all_gather | solution.py:60
  341.6 15.6 %all-gather.3 = f32[4,2,16384]{2,1,0:T(2,128)S(1)} all-gather(f32[1,2,16384]{2,1,0:T(2,128)S(1)} %reshape.445), channel_id=1, replica_groups=mesh['tm_0'=4,'tm_1'=8,'tm_2'=2,'space'=4] {'space'}, dimensions={0}, use_global_device_ids=true | all-gather | bytes 655360 | tf_op jit(solution)/shard_map/all_gather | solution.py:233
  (199 shorter events, 127.6 us)
Async XLA Ops:
  6.5 7.9 %collective-permute-start = (f32[2,128,128]{2,1,0:T(8,128)}, f32[2,128,128]{2,1,0:T(8,128)S(1)}, u32[]{:S(2)}, u32[]{:S(2)}) collective-permute-start(f32[2,128,128]{2,1,0:T(8,128)} %bitcast.636), channel_id=1, source_target_pairs={{0,4},{4,8},{8,12},{12,16},{16,20},{20,24},{24,28},{28,32},{32,36}... | collective-permute-start | bytes 393224 | tf_op jit(solution)/shard_map/ppermute | solution.py:46
  16.5 8.4 %collective-permute-start.1 = (f32[5,1,128,128]{3,2,1,0:T(8,128)S(1)}, f32[5,1,128,128]{3,2,1,0:T(8,128)S(1)}, u32[]{:S(2)}, u32[]{:S(2)}) collective-permute-start(f32[5,1,128,128]{3,2,1,0:T(8,128)S(1)} %get-tuple-element.65), channel_id=1, source_target_pairs={{1,0},{2,1},{3,2},{5,4},{6,5},{7,6},{9,8},{10,9},{11,10},{13,12},{... | collective-permute-start | bytes 983048 | tf_op jit(solution)/shard_map/ppermute | solution.py:22
  19.9 6.1 %collective-permute-start.2 = (f32[5,1,128,128]{3,2,1,0:T(8,128)S(1)}, f32[5,1,128,128]{3,2,1,0:T(8,128)}, u32[]{:S(2)}, u32[]{:S(2)}) collective-permute-start(f32[5,1,128,128]{3,2,1,0:T(8,128)S(1)} %get-tuple-element.66), channel_id=1, source_target_pairs={{0,1},{1,2},{2,3},{4,5},{5,6},{6,7},{8,9},{9,10},{10,11},{12,13},{... | collective-permute-start | bytes 983048 | tf_op jit(solution)/shard_map/ppermute | solution.py:19
  27.6 6.5 %collective-permute-start.3 = (f32[1,128,128]{2,1,0:T(8,128)S(1)}, f32[1,128,128]{2,1,0:T(8,128)S(1)}, u32[]{:S(2)}, u32[]{:S(2)}) collective-permute-start(f32[1,128,128]{2,1,0:T(8,128)S(1)} %get-tuple-element.95), channel_id=1, source_target_pairs={{1,0},{2,1},{3,2},{5,4},{6,5},{7,6},{9,8},{10,9},{11,10},{13,12},{... | collective-permute-start | bytes 196616 | tf_op jit(solution)/shard_map/ppermute | solution.py:22
  29.5 5.8 %collective-permute-start.4 = (f32[1,128,128]{2,1,0:T(8,128)S(1)}, f32[1,128,128]{2,1,0:T(8,128)S(1)}, u32[]{:S(2)}, u32[]{:S(2)}) collective-permute-start(f32[1,128,128]{2,1,0:T(8,128)S(1)} %get-tuple-element.96), channel_id=1, source_target_pairs={{0,1},{1,2},{2,3},{4,5},{5,6},{6,7},{8,9},{9,10},{10,11},{12,13},{... | collective-permute-start | bytes 196616 | tf_op jit(solution)/shard_map/ppermute | solution.py:19
  35.5 6.3 %collective-permute-start.5 = (f32[1,128,128]{2,1,0:T(8,128)S(1)}, f32[1,128,128]{2,1,0:T(8,128)S(1)}, u32[]{:S(2)}, u32[]{:S(2)}) collective-permute-start(f32[1,128,128]{2,1,0:T(8,128)S(1)} %get-tuple-element.93), channel_id=1, source_target_pairs={{1,0},{2,1},{3,2},{5,4},{6,5},{7,6},{9,8},{10,9},{11,10},{13,12},{... | collective-permute-start | bytes 196616 | tf_op jit(solution)/shard_map/ppermute | solution.py:22
  43.2 6.3 %collective-permute-start.7 = (f32[1,128,128]{2,1,0:T(8,128)S(1)}, f32[1,128,128]{2,1,0:T(8,128)S(1)}, u32[]{:S(2)}, u32[]{:S(2)}) collective-permute-start(f32[1,128,128]{2,1,0:T(8,128)S(1)} %get-tuple-element.91), channel_id=1, source_target_pairs={{1,0},{2,1},{3,2},{5,4},{6,5},{7,6},{9,8},{10,9},{11,10},{13,12},{... | collective-permute-start | bytes 196616 | tf_op jit(solution)/shard_map/ppermute | solution.py:22
  50.9 6.2 %collective-permute-start.9 = (f32[1,128,128]{2,1,0:T(8,128)S(1)}, f32[1,128,128]{2,1,0:T(8,128)S(1)}, u32[]{:S(2)}, u32[]{:S(2)}) collective-permute-start(f32[1,128,128]{2,1,0:T(8,128)S(1)} %get-tuple-element.89), channel_id=1, source_target_pairs={{1,0},{2,1},{3,2},{5,4},{6,5},{7,6},{9,8},{10,9},{11,10},{13,12},{... | collective-permute-start | bytes 196616 | tf_op jit(solution)/shard_map/ppermute | solution.py:22
  58.6 6.3 %collective-permute-start.11 = (f32[1,128,128]{2,1,0:T(8,128)S(1)}, f32[1,128,128]{2,1,0:T(8,128)S(1)}, u32[]{:S(2)}, u32[]{:S(2)}) collective-permute-start(f32[1,128,128]{2,1,0:T(8,128)S(1)} %get-tuple-element.87), channel_id=1, source_target_pairs={{1,0},{2,1},{3,2},{5,4},{6,5},{7,6},{9,8},{10,9},{11,10},{13,12},{... | collective-permute-start | bytes 196616 | tf_op jit(solution)/shard_map/ppermute | solution.py:22
  68.5 17.1 %all-to-all-start.1 = ((f32[4,2,16384]{2,1,0:T(2,128)}), f32[4,2,16384]{2,1,0:T(2,128)S(1)}, u32[]{:S(2)}, u32[]{:S(2)}) async-start(f32[4,2,16384]{2,1,0:T(2,128)} %broadcast_in_dim.23), calls=%async_computation.1 | async-start | bytes 1048576 | tf_op jit(solution)/shard_map/all_to_all | solution.py:29
  72.5 59.1 %all-gather.8.cloned.1.call-start = ((), (), s32[]{:S(2)}) async-start(), calls=%async_computation.3 | async-start | bytes 1179648 | tf_op jit(solution)/shard_map/all_gather | solution.py:60
  94.0 76.2 %all-gather.10.cloned.1.call-start = ((), (), s32[]{:S(2)}) async-start(), calls=%async_computation.4 | async-start | bytes 1179648 | tf_op jit(solution)/shard_map/all_gather | solution.py:60
  97.0 12.7 %all-to-all-start = ((f32[4,2,16384]{2,1,0:T(2,128)}), f32[4,2,16384]{2,1,0:T(2,128)S(1)}, u32[]{:S(2)}, u32[]{:S(2)}) async-start(f32[4,2,16384]{2,1,0:T(2,128)} %broadcast_in_dim.21), calls=%async_computation | async-start | bytes 1048576 | tf_op jit(solution)/shard_map/all_to_all | solution.py:29
  101.9 227.5 %all-gather.12.cloned.1.call-start = ((), (), s32[]{:S(2)}) async-start(), calls=%async_computation.5 | async-start | bytes 1179648 | tf_op jit(solution)/shard_map/all_gather | solution.py:60
  210.0 6.3 %collective-permute-start.15 = (f32[1,128,128]{2,1,0:T(8,128)S(1)}, f32[1,128,128]{2,1,0:T(8,128)S(1)}, u32[]{:S(2)}, u32[]{:S(2)}) collective-permute-start(f32[1,128,128]{2,1,0:T(8,128)S(1)} %get-tuple-element.83), channel_id=1, source_target_pairs={{1,0},{2,1},{3,2},{5,4},{6,5},{7,6},{9,8},{10,9},{11,10},{13,12},{... | collective-permute-start | bytes 196616 | tf_op jit(solution)/shard_map/ppermute | solution.py:22
  218.0 6.2 %collective-permute-start.17 = (f32[2,128,128]{2,1,0:T(8,128)S(1)}, f32[2,128,128]{2,1,0:T(8,128)S(1)}, u32[]{:S(2)}, u32[]{:S(2)}) collective-permute-start(f32[2,128,128]{2,1,0:T(8,128)S(1)} %get-tuple-element.46), channel_id=1, source_target_pairs={{0,4},{4,8},{8,12},{12,16},{16,20},{20,24},{24,28},{28,32},{32,36}... | collective-permute-start | bytes 393224 | tf_op jit(solution)/shard_map/ppermute | solution.py:46
  224.4 9.3 %collective-permute-start.18 = (f32[5,1,128,128]{3,2,1,0:T(8,128)S(1)}, f32[5,1,128,128]{3,2,1,0:T(8,128)S(1)}, u32[]{:S(2)}, u32[]{:S(2)}) collective-permute-start(f32[5,1,128,128]{3,2,1,0:T(8,128)S(1)} %get-tuple-element.63), channel_id=1, source_target_pairs={{1,0},{2,1},{3,2},{5,4},{6,5},{7,6},{9,8},{10,9},{11,10},{13,12},{... | collective-permute-start | bytes 983048 | tf_op jit(solution)/shard_map/ppermute | solution.py:22
  226.3 8.5 %collective-permute-start.19 = (f32[5,1,128,128]{3,2,1,0:T(8,128)S(1)}, f32[5,1,128,128]{3,2,1,0:T(8,128)S(1)}, u32[]{:S(2)}, u32[]{:S(2)}) collective-permute-start(f32[5,1,128,128]{3,2,1,0:T(8,128)S(1)} %get-tuple-element.64), channel_id=1, source_target_pairs={{0,1},{1,2},{2,3},{4,5},{5,6},{6,7},{8,9},{9,10},{10,11},{12,13},{... | collective-permute-start | bytes 983048 | tf_op jit(solution)/shard_map/ppermute | solution.py:19
  235.4 6.3 %collective-permute-start.20 = (f32[1,128,128]{2,1,0:T(8,128)S(1)}, f32[1,128,128]{2,1,0:T(8,128)S(1)}, u32[]{:S(2)}, u32[]{:S(2)}) collective-permute-start(f32[1,128,128]{2,1,0:T(8,128)S(1)} %get-tuple-element.81), channel_id=1, source_target_pairs={{1,0},{2,1},{3,2},{5,4},{6,5},{7,6},{9,8},{10,9},{11,10},{13,12},{... | collective-permute-start | bytes 196616 | tf_op jit(solution)/shard_map/ppermute | solution.py:22
  243.2 6.2 %collective-permute-start.22 = (f32[1,128,128]{2,1,0:T(8,128)S(1)}, f32[1,128,128]{2,1,0:T(8,128)S(1)}, u32[]{:S(2)}, u32[]{:S(2)}) collective-permute-start(f32[1,128,128]{2,1,0:T(8,128)S(1)} %get-tuple-element.79), channel_id=1, source_target_pairs={{1,0},{2,1},{3,2},{5,4},{6,5},{7,6},{9,8},{10,9},{11,10},{13,12},{... | collective-permute-start | bytes 196616 | tf_op jit(solution)/shard_map/ppermute | solution.py:22
  250.9 6.2 %collective-permute-start.24 = (f32[1,128,128]{2,1,0:T(8,128)S(1)}, f32[1,128,128]{2,1,0:T(8,128)S(1)}, u32[]{:S(2)}, u32[]{:S(2)}) collective-permute-start(f32[1,128,128]{2,1,0:T(8,128)S(1)} %get-tuple-element.77), channel_id=1, source_target_pairs={{1,0},{2,1},{3,2},{5,4},{6,5},{7,6},{9,8},{10,9},{11,10},{13,12},{... | collective-permute-start | bytes 196616 | tf_op jit(solution)/shard_map/ppermute | solution.py:22
  258.5 6.2 %collective-permute-start.26 = (f32[1,128,128]{2,1,0:T(8,128)S(1)}, f32[1,128,128]{2,1,0:T(8,128)S(1)}, u32[]{:S(2)}, u32[]{:S(2)}) collective-permute-start(f32[1,128,128]{2,1,0:T(8,128)S(1)} %get-tuple-element.75), channel_id=1, source_target_pairs={{1,0},{2,1},{3,2},{5,4},{6,5},{7,6},{9,8},{10,9},{11,10},{13,12},{... | collective-permute-start | bytes 196616 | tf_op jit(solution)/shard_map/ppermute | solution.py:22
  266.3 6.3 %collective-permute-start.28 = (f32[1,128,128]{2,1,0:T(8,128)S(1)}, f32[1,128,128]{2,1,0:T(8,128)S(1)}, u32[]{:S(2)}, u32[]{:S(2)}) collective-permute-start(f32[1,128,128]{2,1,0:T(8,128)S(1)} %get-tuple-element.73), channel_id=1, source_target_pairs={{1,0},{2,1},{3,2},{5,4},{6,5},{7,6},{9,8},{10,9},{11,10},{13,12},{... | collective-permute-start | bytes 196616 | tf_op jit(solution)/shard_map/ppermute | solution.py:22
  366.5 6.2 %collective-permute-start.32 = (f32[1,128,128]{2,1,0:T(8,128)S(1)}, f32[1,128,128]{2,1,0:T(8,128)S(1)}, u32[]{:S(2)}, u32[]{:S(2)}) collective-permute-start(f32[1,128,128]{2,1,0:T(8,128)S(1)} %get-tuple-element.69), channel_id=1, source_target_pairs={{1,0},{2,1},{3,2},{5,4},{6,5},{7,6},{9,8},{10,9},{11,10},{13,12},{... | collective-permute-start | bytes 196616 | tf_op jit(solution)/shard_map/ppermute | solution.py:22
  (37 other events, 432.5 us)
Sparse Core Ops, SparseCore 0:
  94.2 37.4 all-gather.7
  133.4 36.7 all-gather.9
  296.6 32.7 all-gather.11
where the time goes:
time: 383 us; the launch traced here: 382 us
  waiting for transfers between devices  119 us (31%)
  starting transfers between devices  117 us (31%)
  blocking collectives  101 us (26%)
  between operations  14.9 us (4%)
  other arithmetic  11.9 us (3%)
  matrix products  10.6 us (3%)
  local copies, waits for them, and re-layouts  7.85 us (2%)
    all_gather x3, waiting for transfers between devices, carried_in(): pieces = jax.tree.map(lambda part: lax.all_gather(part, axis), subtotal)  80.7 us
    ppermute x16, starting transfers between devices, with_halo(): lax.ppermute(lax.slice_in_dim(block, block.shape[dim] - width, None, axis...  65.3 us
    all_gather x6, blocking collectives, carried_in(): pieces = jax.tree.map(lambda part: lax.all_gather(part, axis), subtotal)  58.1 us
    ppermute x16, starting transfers between devices, with_halo(): lax.ppermute(lax.slice_in_dim(block, 0, width, axis=dim), axis, backward)  32.5 us
    all_gather x2, blocking collectives, body(): lax.all_gather(inverse_flat, 'space', axis=0, tiled=True)  31.4 us
    ppermute x16, waiting for transfers between devices, with_halo(): lax.ppermute(lax.slice_in_dim(block, block.shape[dim] - width, None, axis...  20.2 us
    all_to_all x1, blocking collectives, copy_for_each(): lax.all_to_all(jnp.broadcast_to(x[None], (devices, *x.shape)), axis, 0, 0...  11.6 us
    ppermute x2, starting transfers between devices, shifted(): lax.ppermute(value, axis, [(source, source + steps) for source in range(f...  9.96 us
  transfers between devices with their start and end apart: 39, of which 24 were waited for; matrix products, arithmetic and copies ran while one was open for 1% of the time, Pallas kernels for 0%

commit v1 on v0

v1 whole, which is shorter than its diff:
```python
import functools
import math

import jax
import jax.numpy as jnp
import numpy as np
from jax import lax
from jax.experimental import pallas as pl
from jax.experimental.pallas import tpu as pltpu
from jax.sharding import PartitionSpec as P

MESH = pl.DeviceIdType.MESH
GROUPS = 4


def node_tables():
    radical = math.sqrt(3.0 / 7.0)
    times = [0.0, (1.0 - radical) / 2.0, 0.5, (1.0 + radical) / 2.0, 1.0]
    integrals = np.zeros((4, 5))
    for column in range(5):
        coeffs = np.array([1.0])
        for other in range(5):
            if other != column:
                coeffs = np.convolve(coeffs, [-times[other], 1.0]) / (times[column] - times[other])
        powers = np.arange(1, 6)
        for section in range(4):
            integrals[section, column] = np.sum(
                coeffs * (times[section + 1] ** powers - times[section] ** powers) / powers
            )
    coarse = [0.0, 0.5, 1.0]
    interp = np.zeros((5, 3))
    for column in range(3):
        for section in range(5):
            weight = 1.0
            for other in range(3):
                if other != column:
                    weight *= (times[section] - coarse[other]) / (coarse[column] - coarse[other])
            interp[section, column] = weight
    return times, integrals, interp


TIMES, QUAD, INTERP = node_tables()
SPACING = [TIMES[m + 1] - TIMES[m] for m in range(4)]


def mixed(weights, values):
    total = None
    for weight, value in zip(weights, values):
        if value is None or abs(weight) < 1e-14:
            continue
        term = float(weight) * value
        total = term if total is None else total + term
    return total


def sweep(u, q, mu):
    v = [u[0]]
    for m in range(4):
        weights = list(QUAD[m])
        weights[m] -= SPACING[m]
        rate = mixed(weights + [SPACING[m]], u + [v[m]])
        new = -mu * rate
        if q is not None:
            new = new + q[m]
        if v[m] is not None:
            new = new + v[m]
        v.append(new)
    return v


def coarse_terms(v, q, mu):
    weights = QUAD[0] + QUAD[1]
    weights[0] -= 0.5
    left = -mu * mixed(weights, v)
    weights = QUAD[2] + QUAD[3]
    weights[2] -= 0.5
    right = -mu * mixed(weights, v)
    if q is not None:
        left = left + (q[0] + q[1])
        right = right + (q[2] + q[3])
    return left, right


def sources(q, guess, before, mu):
    rho = 1.0 - 0.5 * mu
    v = sweep([before, guess, guess, guess, guess], q, mu)
    left, right = coarse_terms(v, q, mu)
    forced = rho * left + right
    u = [None, None, left, None, forced]
    for m in (1, 3):
        u[m] = v[m] + mixed(INTERP[m], [-before, left - v[2], forced - v[4]])
    v = sweep(u, q, mu)
    left2, right2 = coarse_terms(v, q, mu)
    return forced, v, left2, rho * left2 + right2


def responses(mu):
    rho = 1.0 - 0.5 * mu
    square = rho * rho
    u = [1.0, None, rho, None, square]
    for m in (1, 3):
        u[m] = float(INTERP[m, 0]) + float(INTERP[m, 1]) * rho + float(INTERP[m, 2]) * square
    v = sweep(u, None, mu)
    left, right = coarse_terms(v, None, mu)
    return rho, square, v, left, rho * left + right


def sine(length):
    k = np.arange(1, length + 1)
    return math.sqrt(2.0 / (length + 1)) * np.sin(math.pi / (length + 1) * np.outer(k, k))


def eigen(length):
    return 2.0 - 2.0 * np.cos(math.pi / (length + 1) * np.arange(1, length + 1))


def along_z(planes, matrix):
    n = len(planes)
    half = n // 2
    even = [planes[i] + planes[n - 1 - i] for i in range(half)]
    odd = [planes[i] - planes[n - 1 - i] for i in range(half)]
    out = []
    for k in range(n):
        out.append(mixed(matrix[k][:half], even if k % 2 == 0 else odd))
    return out


def kernel(
    sizes, start_hbm, force_hbm, first_hbm, step_ref, sin_ref, lamxy_ref, out_hbm,
    f_raw, g_raw, i_raw, b_raw, hat, recv, lam, spec, fb, keep, steps, scan_in, gains, gain_all,
    prefix, totals, cd, beta, yout, outr, res,
    load_sem, store_sem, in_send, in_recv, shift_sem, step_send, step_recv, scan_send, scan_recv,
    gain_send, gain_recv, tot_send, tot_recv, back_send, back_recv, out_send, out_recv,
):
    count, spaces, nx, ny, nz = sizes
    per = count // GROUPS
    depth = nz // spaces
    cols = nx // spaces
    rows = nz * cols
    part = rows // per
    high = lax.Precision.HIGHEST
    tm = lax.axis_index("tm")
    sp = lax.axis_index("space")
    group = tm // per
    slot = tm % per

    def dot(a, b):
        return jnp.dot(a, b, precision=high, preferred_element_type=jnp.float32)

    loads = [
        pltpu.make_async_copy(force_hbm.at[0], f_raw, load_sem.at[0]),
        pltpu.make_async_copy(start_hbm.at[0], g_raw, load_sem.at[1]),
        pltpu.make_async_copy(first_hbm, i_raw, load_sem.at[2]),
    ]
    for load in loads:
        load.start()

    barrier = pltpu.get_barrier_semaphore()

    def greet(target):
        pl.semaphore_signal(barrier, inc=1, device_id=target, device_id_type=MESH)

    following = (lax.rem(tm + 1, count), sp)
    preceding = (lax.rem(tm + count - 1, count), sp)
    for d in range(1, spaces):
        greet((tm, lax.rem(sp + d, spaces)))
    for d in range(1, per):
        greet((group * per + lax.rem(slot + d, per), sp))
    for d in range(1, GROUPS):
        greet((lax.rem(group + d, GROUPS) * per + slot, sp))
    greet(following)
    greet(preceding)

    step = step_ref[0]
    z_eigen = eigen(nz)
    here = lamxy_ref[pl.ds(pl.multiple_of(sp * cols, cols), cols), :]
    for k in range(nz):
        lam[pl.ds(k * cols, cols), :] = here + float(z_eigen[k])
    steps[slot] = jnp.full((8, ny), step, jnp.float32)

    pl.semaphore_wait(barrier, spaces + per + GROUPS - 1)

    for load in loads:
        load.wait()
    shift = pltpu.make_async_remote_copy(
        src_ref=g_raw, dst_ref=b_raw, send_sem=shift_sem.at[0], recv_sem=shift_sem.at[1],
        device_id=following, device_id_type=MESH,
    )
    shift.start()
    step_copies = []
    for d in range(1, per):
        copy = pltpu.make_async_remote_copy(
            src_ref=steps.at[slot], dst_ref=steps.at[slot],
            send_sem=step_send.at[d - 1], recv_sem=step_recv.at[d - 1],
            device_id=(group * per + lax.rem(slot + d, per), sp), device_id_type=MESH,
        )
        copy.start()
        step_copies.append(copy)

    in_copies = []

    def hand_out(f):
        mine = pl.multiple_of(sp * cols, cols)
        recv[f, pl.ds(sp * depth, depth)] = hat[f, :, pl.ds(mine, cols), :]
        for d in range(1, spaces):
            other = lax.rem(sp + d, spaces)
            copy = pltpu.make_async_remote_copy(
                src_ref=hat.at[f, :, pl.ds(pl.multiple_of(other * cols, cols), cols), :],
                dst_ref=recv.at[f, pl.ds(sp * depth, depth)],
                send_sem=in_send.at[f, d - 1], recv_sem=in_recv.at[f, d - 1],
                device_id=(tm, other), device_id_type=MESH,
            )
            copy.start()
            in_copies.append(copy)

    for m in range(4):
        for z in range(depth):
            q = step * mixed(QUAD[m], [f_raw[j, z] for j in range(5)])
            hat[m, z] = dot(dot(sin_ref[...], q), sin_ref[...])
        hand_out(m)
    for z in range(depth):
        hat[4, z] = dot(dot(sin_ref[...], g_raw[z]), sin_ref[...])
    hand_out(4)
    shift.wait_recv()
    for z in range(depth):
        before = jnp.where(tm == 0, i_raw[z], b_raw[z])
        hat[5, z] = dot(dot(sin_ref[...], before), sin_ref[...])
    hand_out(5)

    z_matrix = sine(nz)
    for copy in step_copies:
        copy.wait_recv()

    share = pl.ds(pl.multiple_of(slot * part, part), part)

    def slice_gain(i, carry):
        total_g, total_a = carry
        keep_g, keep_a = total_g, total_a
        mu = steps[i, 0:1, :] * lam[share, :]
        _, square, _, _, a = responses(mu)
        prefix[i, 0] = keep_g
        prefix[i, 1] = keep_a
        gains[i, 0] = square
        gains[i, 1] = a
        return square * total_g, square * total_a + a * total_g

    ones = jnp.ones((part, ny), jnp.float32)
    total_g, total_a = lax.fori_loop(0, per, slice_gain, (ones, jnp.zeros_like(ones)))
    gain_all[group, 0] = total_g
    gain_all[group, 1] = total_a
    gain_copies = []
    for d in range(1, GROUPS):
        copy = pltpu.make_async_remote_copy(
            src_ref=gain_all.at[group], dst_ref=gain_all.at[group],
            send_sem=gain_send.at[d - 1], recv_sem=gain_recv.at[d - 1],
            device_id=(lax.rem(group + d, GROUPS) * per + slot, sp), device_id_type=MESH,
        )
        copy.start()
        gain_copies.append(copy)

    for f in range(6):
        for d in range(1, spaces):
            in_copies[f * (spaces - 1) + d - 1].wait_recv()
        planes = along_z([recv[f, z] for z in range(nz)], z_matrix)
        for k in range(nz):
            spec[f, pl.ds(k * cols, cols), :] = planes[k]

    block = 32

    def pre(i, carry):
        at = pl.ds(pl.multiple_of(i * block, block), block)
        mu = step * lam[at, :]
        q = [spec[m, at, :] for m in range(4)]
        before = spec[5, at, :]
        forced, v, left, forced2 = sources(q, spec[4, at, :], before, mu)
        keep[0, at, :] = v[1]
        keep[1, at, :] = v[2]
        keep[2, at, :] = v[3]
        keep[3, at, :] = v[4]
        keep[4, at, :] = left
        keep[5, at, :] = forced2
        _, square, _, _, a = responses(mu)
        start = jnp.where(tm == 0, before, 0.0)
        fb[0, at, :] = forced + square * start
        fb[1, at, :] = forced2 + (square + a) * start
        return carry

    lax.fori_loop(0, rows // block, pre, 0)

    scan_copies = []
    for d in range(1, per):
        other = lax.rem(slot + d, per)
        copy = pltpu.make_async_remote_copy(
            src_ref=fb.at[:, pl.ds(pl.multiple_of(other * part, part), part), :],
            dst_ref=scan_in.at[slot],
            send_sem=scan_send.at[d - 1], recv_sem=scan_recv.at[d - 1],
            device_id=(group * per + other, sp), device_id_type=MESH,
        )
        copy.start()
        scan_copies.append(copy)
    scan_in[slot] = fb[:, share, :]

    def post(i, carry):
        at = pl.ds(pl.multiple_of(i * block, block), block)
        mu = step * lam[at, :]
        rho, square, v, left, a = responses(mu)
        va = [None, keep[0, at, :], keep[1, at, :], keep[2, at, :], keep[3, at, :]]
        lefta = keep[4, at, :]
        forceda = keep[5, at, :]
        beta[0, 0, at, :] = lefta
        beta[0, 1, at, :] = left
        beta[0, 2, at, :] = rho
        beta[1, 0, at, :] = forceda
        beta[1, 1, at, :] = a
        beta[1, 2, at, :] = square
        for n, m in enumerate((1, 3)):
            w = [float(x) for x in INTERP[m]]
            beta[2 + n, 0, at, :] = va[m] + w[1] * (lefta - va[2]) + w[2] * (forceda - va[4])
            beta[2 + n, 1, at, :] = v[m] - w[0] + w[1] * (left - v[2]) + w[2] * (a - v[4])
            beta[2 + n, 2, at, :] = w[0] + w[1] * rho + w[2] * square
        return carry

    lax.fori_loop(0, rows // block, post, 0)

    for copy in scan_copies:
        copy.wait_recv()
    zero = jnp.zeros((part, ny), jnp.float32)

    def advance(i, carry):
        c, d = carry
        f, b = scan_in[i, 0], scan_in[i, 1]
        scan_in[i, 0] = c
        scan_in[i, 1] = d
        g, a = gains[i, 0], gains[i, 1]
        return g * c + f, g * d + (a * c + b)

    c, d = lax.fori_loop(0, per, advance, (zero, zero))
    totals[group, 0] = c
    totals[group, 1] = d
    tot_copies = []
    for n in range(1, GROUPS):
        copy = pltpu.make_async_remote_copy(
            src_ref=totals.at[group], dst_ref=totals.at[group],
            send_sem=tot_send.at[n - 1], recv_sem=tot_recv.at[n - 1],
            device_id=(lax.rem(group + n, GROUPS) * per + slot, sp), device_id_type=MESH,
        )
        copy.start()
        tot_copies.append(copy)
    for copy in gain_copies:
        copy.wait_recv()
    for copy in tot_copies:
        copy.wait_recv()
    c, d = zero, zero
    start_c, start_d = zero, zero
    for other in range(GROUPS - 1):
        g, a = gain_all[other, 0], gain_all[other, 1]
        c, d = g * c + totals[other, 0], g * d + (a * c + totals[other, 1])
        start_c = jnp.where(group == other + 1, c, start_c)
        start_d = jnp.where(group == other + 1, d, start_d)

    for i in range(per):
        g, a = prefix[i, 0], prefix[i, 1]
        prefix[i, 0] = scan_in[i, 0] + g * start_c
        prefix[i, 1] = scan_in[i, 1] + (g * start_d + a * start_c)

    back_copies = []
    for d in range(1, per):
        other = lax.rem(slot + d, per)
        copy = pltpu.make_async_remote_copy(
            src_ref=prefix.at[other], dst_ref=cd.at[:, share, :],
            send_sem=back_send.at[d - 1], recv_sem=back_recv.at[d - 1],
            device_id=(group * per + other, sp), device_id_type=MESH,
        )
        copy.start()
        back_copies.append(copy)
    cd[:, share, :] = prefix[slot]
    for copy in back_copies:
        copy.wait_recv()

    out_copies = []
    for m in (0, 4, 2, 1, 3):
        for r in range(0, cols, 8):
            planes = []
            for k in range(nz):
                at = pl.ds(k * cols + r, 8)
                before = spec[5, at, :]
                c = jnp.where(tm == 0, before, cd[0, at, :])
                d = jnp.where(tm == 0, before, cd[1, at, :])
                if m == 0:
                    planes.append(d)
                else:
                    n = {2: 0, 4: 1, 1: 2, 3: 3}[m]
                    planes.append(beta[n, 0, at, :] + beta[n, 1, at, :] * c + beta[n, 2, at, :] * d)
            planes = along_z(planes, z_matrix)
            for z in range(nz):
                spec_at = pl.ds(z * cols + r, 8)
                yout[m, spec_at, :] = planes[z]
        yout[m] = dot(yout[m], sin_ref[...])
        mine = pl.ds(pl.multiple_of(sp * cols, cols), cols)
        for d in range(1, spaces):
            other = lax.rem(sp + d, spaces)
            for z in range(depth):
                copy = pltpu.make_async_remote_copy(
                    src_ref=yout.at[m, pl.ds(pl.multiple_of((other * depth + z) * cols, cols), cols), :],
                    dst_ref=outr.at[m, z, mine, :],
                    send_sem=out_send.at[m, d - 1, z], recv_sem=out_recv.at[m, d - 1, z],
                    device_id=(tm, other), device_id_type=MESH,
                )
                copy.start()
                out_copies.append(copy)
        for z in range(depth):
            outr[m, z, mine, :] = yout[m, pl.ds(pl.multiple_of((sp * depth + z) * cols, cols), cols), :]

    stores = []
    each = (spaces - 1) * depth
    for n, m in enumerate((0, 4, 2, 1, 3)):
        for copy in out_copies[n * each : (n + 1) * each]:
            copy.wait_recv()
        for z in range(depth):
            res[m, z] = dot(sin_ref[...], outr[m, z])
        store = pltpu.make_async_copy(res.at[m], out_hbm.at[0, m], store_sem.at[m])
        store.start()
        stores.append(store)
    for copy in [shift] + step_copies + in_copies + gain_copies + scan_copies + tot_copies + back_copies + out_copies:
        copy.wait_send()
    for store in stores:
        store.wait()


def body(sizes, initial, start_guess, forcing, step_size):
    count, spaces, nx, ny, nz = sizes
    per = count // GROUPS
    depth = nz // spaces
    cols = nx // spaces
    rows = nz * cols
    part = rows // per
    table = jnp.asarray(sine(nx), jnp.float32)
    lamxy = jnp.asarray(eigen(nx)[:, None] + eigen(ny)[None, :], jnp.float32)
    vmem = pl.BlockSpec(memory_space=pltpu.VMEM)
    hbm = pl.BlockSpec(memory_space=pl.ANY)
    f32 = lambda *shape: pltpu.VMEM(shape, jnp.float32)
    dma = lambda *shape: pltpu.SemaphoreType.DMA(shape)
    return pl.pallas_call(
        functools.partial(kernel, sizes),
        out_shape=jax.ShapeDtypeStruct((1, 5, depth, nx, ny), jnp.float32),
        in_specs=[hbm, hbm, hbm, pl.BlockSpec(memory_space=pltpu.SMEM), vmem, vmem],
        out_specs=hbm,
        scratch_shapes=[
            f32(5, depth, nx, ny), f32(depth, nx, ny), f32(depth, nx, ny), f32(depth, nx, ny),
            f32(6, depth, nx, ny), f32(6, nz, cols, ny), f32(rows, ny), f32(6, rows, ny),
            f32(2, rows, ny), f32(6, rows, ny), f32(per, 8, ny), f32(per, 2, part, ny),
            f32(per, 2, part, ny), f32(GROUPS, 2, part, ny), f32(per, 2, part, ny),
            f32(GROUPS, 2, part, ny), f32(2, rows, ny), f32(4, 3, rows, ny), f32(5, rows, ny),
            f32(5, depth, nx, ny), f32(5, depth, nx, ny),
            dma(3), dma(5), dma(6, spaces - 1), dma(6, spaces - 1), dma(2), dma(per - 1), dma(per - 1),
            dma(per - 1), dma(per - 1), dma(GROUPS - 1), dma(GROUPS - 1), dma(GROUPS - 1), dma(GROUPS - 1),
            dma(per - 1), dma(per - 1), dma(5, spaces - 1, depth), dma(5, spaces - 1, depth),
        ],
        compiler_params=pltpu.CompilerParams(collective_id=0, has_side_effects=True),
    )(start_guess, forcing, initial, step_size, table, lamxy)


def solution(mesh):
    sizes = (mesh.shape["tm"], mesh.shape["space"], 128, 128, 8)
    placed = (
        P("space", None, None),
        P("tm", "space", None, None),
        P("tm", None, "space", None, None),
        P("tm"),
    )
    return jax.shard_map(
        functools.partial(body, sizes),
        mesh=mesh,
        in_specs=placed,
        out_specs=P("tm", None, "space", None, None),
        check_vma=False,
    )
```

time: 383 us -> 61 us (0.16)
  waiting for transfers between devices: 119 us -> 0 us
  starting transfers between devices: 117 us -> 0 us
  blocking collectives: 101 us -> 0 us
  Pallas kernels: 0 us -> 58.2 us
  between operations: 14.9 us -> 0.66 us
  other arithmetic: 11.9 us -> 0 us
  matrix products: 10.6 us -> 0 us
  local copies, waits for them, and re-layouts: 7.85 us -> 1.97 us
    ppermute x34 -> x0, starting transfers between devices: 108 us -> none  [the longest x16 65.3 us: with_halo(): lax.ppermute(lax.slice_in_dim(block, block.shape[dim] - width, None, axis...]
    all_gather x8 -> x0, blocking collectives: 89.4 us -> none  [the longest x6 58.1 us: carried_in(): pieces = jax.tree.map(lambda part: lax.all_gather(part, axis), subtotal)]
    all_gather x3 -> x0, waiting for transfers between devices: 80.7 us -> none  [carried_in(): pieces = jax.tree.map(lambda part: lax.all_gather(part, axis), subtotal)]
    pallas_call x0 -> x1, Pallas kernels: none -> 58.2 us  [body(): pl.pallas_call(functools.partial(kernel, sizes), out_shape=jax.ShapeDtype...]
    ppermute x34 -> x0, waiting for transfers between devices: 29.4 us -> none  [the longest x16 20.2 us: with_halo(): lax.ppermute(lax.slice_in_dim(block, block.shape[dim] - width, None, axis...]
    all_to_all x1 -> x0, blocking collectives: 11.6 us -> none  [copy_for_each(): lax.all_to_all(jnp.broadcast_to(x[None], (devices, *x.shape)), axis, 0, 0...]
    dot_general x15 -> x0, matrix products: 10.6 us -> none  [the longest x5 3.18 us: lateral(): mixed = jnp.einsum('ai,zij->zaj', x_matrix, field, precision=highest)]
    all_to_all x2 -> x0, starting transfers between devices: 8.9 us -> none  [copy_for_each(): lax.all_to_all(jnp.broadcast_to(x[None], (devices, *x.shape)), axis, 0, 0...]
  transfers between devices with their start and end apart: 39 -> 0, of which waited for: 24 -> 0; matrix products, arithmetic and copies ran while one was open for 1% -> 0% of each run, Pallas kernels for 0% -> 0%
where the time goes in v1:
time: 61 us; the launch traced here: 60.8 us
  Pallas kernels  58.2 us (95%)
  local copies, waits for them, and re-layouts  1.97 us (3%)
  between operations  0.66 us (1%)
    pallas_call x1, Pallas kernels, body(): pl.pallas_call(functools.partial(kernel, sizes), out_shape=jax.ShapeDtype...  58.2 us
    unnamed x1, local copies, waits for them, and re-layouts  1.97 us

profile of v1, /device:TPU:1, one launch (start us, length us, event | category | flops | bytes accessed | tf_op | source)
XLA Modules:
  0.0 60.8 jit_solution(2321433645506180769)
XLA Ops:
  0.7 58.2 %shard_map.64 = f32[1,5,2,128,128]{4,3,2,1,0:T(8,128)} custom-call(f32[1,2,128,128]{3,2,1,0:T(8,128)} %start_hbm.1, f32[1,5,2,128,128]{4,3,2,1,0:T(8,128)} %force_hbm.1, f32[2,128,128]{2,1,0:T(8,128)} %first_hbm.1, f32[1]{0:T(128)S(6)} %copy.8.step_ref, f32[128,128]{1,0:T(8,128)} %constant.4.clone.sin_ref, f32[128,128]{1,0:T(8,128)} %constant.5.clone.lamxy_ref), custom_call_target="tpu_custom_call" | custom-call | tf_op jit(solution)/shard_map/pallas_call | solution.py:443
  58.8 2.0 %copy.9 = f32[1,5,2,128,128]{4,3,2,1,0:T(8,128)} copy(f32[1,5,2,128,128]{4,3,2,1,0:T(8,128)} %shard_map.64) | data formatting | bytes 1310720

commit v2 on v1

v2 whole, which is shorter than its diff:
```python
import functools
import math

import jax
import jax.numpy as jnp
import numpy as np
from jax import lax
from jax.experimental import pallas as pl
from jax.experimental.pallas import tpu as pltpu
from jax.sharding import PartitionSpec as P

MESH = pl.DeviceIdType.MESH
GROUPS = 4
RING = 8
PLANES = 8
SPACES = 4
OWNERS = 2 * SPACES
DEPTH = PLANES // SPACES
WIDTH = 128
COLS = WIDTH // OWNERS
SUB = 8
CHUNKS = COLS // SUB
ROWS = PLANES * SUB


def node_tables():
    radical = math.sqrt(3.0 / 7.0)
    times = [0.0, (1.0 - radical) / 2.0, 0.5, (1.0 + radical) / 2.0, 1.0]
    integrals = np.zeros((4, 5))
    for column in range(5):
        coeffs = np.array([1.0])
        for other in range(5):
            if other != column:
                coeffs = np.convolve(coeffs, [-times[other], 1.0]) / (times[column] - times[other])
        powers = np.arange(1, 6)
        for section in range(4):
            integrals[section, column] = np.sum(
                coeffs * (times[section + 1] ** powers - times[section] ** powers) / powers
            )
    coarse = [0.0, 0.5, 1.0]
    interp = np.zeros((5, 3))
    for column in range(3):
        for section in range(5):
            weight = 1.0
            for other in range(3):
                if other != column:
                    weight *= (times[section] - coarse[other]) / (coarse[column] - coarse[other])
            interp[section, column] = weight
    return times, integrals, interp


TIMES, QUAD, INTERP = node_tables()
SPACING = [TIMES[m + 1] - TIMES[m] for m in range(4)]


def mixed(weights, values):
    total = None
    for weight, value in zip(weights, values):
        if value is None or abs(weight) < 1e-14:
            continue
        term = float(weight) * value
        total = term if total is None else total + term
    return total


def sweep(u, q, mu):
    v = [u[0]]
    for m in range(4):
        weights = list(QUAD[m])
        weights[m] -= SPACING[m]
        rate = mixed(weights + [SPACING[m]], u + [v[m]])
        new = -mu * rate
        if q is not None:
            new = new + q[m]
        if v[m] is not None:
            new = new + v[m]
        v.append(new)
    return v


def coarse_terms(v, q, mu):
    weights = QUAD[0] + QUAD[1]
    weights[0] -= 0.5
    left = -mu * mixed(weights, v)
    weights = QUAD[2] + QUAD[3]
    weights[2] -= 0.5
    right = -mu * mixed(weights, v)
    if q is not None:
        left = left + (q[0] + q[1])
        right = right + (q[2] + q[3])
    return left, right


def sources(q, guess, before, mu):
    rho = 1.0 - 0.5 * mu
    v = sweep([before, guess, guess, guess, guess], q, mu)
    left, right = coarse_terms(v, q, mu)
    forced = rho * left + right
    u = [None, None, left, None, forced]
    for m in (1, 3):
        u[m] = v[m] + mixed(INTERP[m], [-before, left - v[2], forced - v[4]])
    v = sweep(u, q, mu)
    left2, right2 = coarse_terms(v, q, mu)
    return forced, v, left2, rho * left2 + right2


def responses(mu):
    rho = 1.0 - 0.5 * mu
    square = rho * rho
    u = [1.0, None, rho, None, square]
    for m in (1, 3):
        u[m] = float(INTERP[m, 0]) + float(INTERP[m, 1]) * rho + float(INTERP[m, 2]) * square
    v = sweep(u, None, mu)
    left, right = coarse_terms(v, None, mu)
    return rho, square, v, left, rho * left + right


def sine(length):
    k = np.arange(1, length + 1)
    return math.sqrt(2.0 / (length + 1)) * np.sin(math.pi / (length + 1) * np.outer(k, k))


def eigen(length):
    return 2.0 - 2.0 * np.cos(math.pi / (length + 1) * np.arange(1, length + 1))


def along_z(planes, matrix):
    n = len(planes)
    half = n // 2
    even = [planes[i] + planes[n - 1 - i] for i in range(half)]
    odd = [planes[i] - planes[n - 1 - i] for i in range(half)]
    out = []
    for k in range(n):
        out.append(mixed(matrix[k][:half], even if k % 2 == 0 else odd))
    return out


def kernel(
    start_hbm, force_hbm, first_hbm, step_ref, sin_hbm, lamxy_hbm, out_ref,
    f_raw, g_raw, i_raw, sin_ref, lamxy, hat, gin, qin, firsts, ghat, qhat, shifted, lam, tab, alpha,
    pair_steps, all_steps, gains, gain_all, fb, scan_in, totals, back, cd, cd_odd, yout, outr,
    load_sem, g_send, g_recv, q_send, q_recv, r_send, r_recv, i_send, i_recv, shift_sem,
    pstep_sem, step_send, step_recv, scan_send, scan_recv, gain_send, gain_recv, tot_send, tot_recv,
    back_send, back_recv, o_send, o_recv, m_send, m_recv,
):
    high = lax.Precision.HIGHEST
    tm = lax.axis_index("tm")
    sp = lax.axis_index("space")
    pair, half = tm // 2, tm % 2
    group, slot = pair // RING, pair % RING
    own = half * SPACES + sp

    def dot(a, b):
        return jnp.dot(a, b, precision=high, preferred_element_type=jnp.float32)

    def owner(d):
        other = lax.rem(own + d, OWNERS)
        return other, (pair * 2 + other // SPACES, lax.rem(other, SPACES))

    def along_ring(d):
        other = lax.rem(slot + d, RING)
        return other, ((group * RING + other) * 2 + half, sp)

    def across(d):
        return ((lax.rem(group + d, GROUPS) * RING + slot) * 2 + half, sp)

    def send(src, dst, send_sem, recv_sem, target):
        copy = pltpu.make_async_remote_copy(
            src_ref=src, dst_ref=dst, send_sem=send_sem, recv_sem=recv_sem,
            device_id=target, device_id_type=MESH,
        )
        copy.start()
        return copy

    pairs = GROUPS * RING
    following = (lax.rem(pair + 1, pairs) * 2 + half, sp)
    preceding = (lax.rem(pair + pairs - 1, pairs) * 2 + half, sp)
    partner = (pair * 2 + 1 - half, lax.rem(sp + SPACES // 2, SPACES))

    loads = [
        pltpu.make_async_copy(start_hbm.at[0], g_raw, load_sem.at[0]),
        pltpu.make_async_copy(sin_hbm, sin_ref, load_sem.at[1]),
        pltpu.make_async_copy(force_hbm.at[0], f_raw, load_sem.at[2]),
        pltpu.make_async_copy(lamxy_hbm.at[pl.ds(pl.multiple_of(own * COLS, COLS), COLS)], lamxy, load_sem.at[3]),
        pltpu.make_async_copy(first_hbm, i_raw, load_sem.at[4]),
    ]
    for load in loads:
        load.start()

    barrier = pltpu.get_barrier_semaphore()

    def greet(target):
        pl.semaphore_signal(barrier, inc=1, device_id=target, device_id_type=MESH)

    for d in range(1, OWNERS):
        greet(owner(d)[1])
    for d in range(1, RING):
        greet(along_ring(d)[1])
    for d in range(1, GROUPS):
        greet(across(d))
    greet(following)
    greet(preceding)

    step = step_ref[0]
    pair_steps[half] = jnp.full((SUB, WIDTH), step, jnp.float32)
    loads[0].wait()
    loads[1].wait()

    def transform(f, planes):
        for z in range(DEPTH):
            hat[f, z] = dot(dot(sin_ref[...], planes[z]), sin_ref[...])

    transform(4, [g_raw[z] for z in range(DEPTH)])
    loads[2].wait()
    pl.semaphore_wait(barrier, OWNERS + RING + GROUPS - 1)

    mine = pl.ds(pl.multiple_of(own * COLS, COLS), COLS)
    here = pl.ds(sp * DEPTH, DEPTH)

    def slab(other, first, size):
        return pl.ds(pl.multiple_of(other * COLS + first, SUB), size)

    pstep_copy = send(
        pair_steps.at[half], pair_steps.at[half], pstep_sem.at[0], pstep_sem.at[1], partner
    )
    g_copies = []
    for d in range(1, OWNERS):
        other, target = owner(d)
        g_copies.append(send(
            hat.at[4, :, slab(other, 0, COLS), :], gin.at[half, here],
            g_send.at[d - 1], g_recv.at[d - 1], target,
        ))
    gin[half, here] = hat[4, :, mine, :]
    q_copies = []
    for m in range(4):
        planes = [
            step * mixed(QUAD[m], [f_raw[j, z] for j in range(5)]) for z in range(DEPTH)
        ]
        transform(m, planes)
        for d in range(1, OWNERS):
            other, target = owner(d)
            q_copies.append(send(
                hat.at[m, :, slab(other, 0, SUB), :], qin.at[0, half, m, here],
                q_send.at[m, d - 1], q_recv.at[m, d - 1], target,
            ))
    r_copies = []
    for d in range(1, OWNERS):
        other, target = owner(d)
        r_copies.append(send(
            hat.at[pl.ds(0, 4), :, slab(other, SUB, SUB), :], qin.at[1, half, :, here],
            r_send.at[d - 1], r_recv.at[d - 1], target,
        ))
    for h in range(CHUNKS):
        for m in range(4):
            qin[h, half, m, here] = hat[m, :, slab(own, h * SUB, SUB), :]

    for load in loads[3:]:
        load.wait()

    def first_copy(d):
        other = lax.rem(sp + d, SPACES)
        return pltpu.make_async_remote_copy(
            src_ref=hat.at[5, :, slab(half * SPACES + other, 0, COLS), :],
            dst_ref=firsts.at[here], send_sem=i_send.at[d - 1], recv_sem=i_recv.at[d - 1],
            device_id=(tm, other), device_id_type=MESH,
        )

    @pl.when(pair == 0)
    def _():
        transform(5, [i_raw[z] for z in range(DEPTH)])
        for d in range(1, SPACES):
            first_copy(d).start()
        firsts[here] = hat[5, :, mine, :]

    z_matrix = sine(PLANES)
    z_eigen = eigen(PLANES)
    for h in range(CHUNKS):
        for k in range(PLANES):
            lam[h, pl.ds(k * SUB, SUB), :] = lamxy[pl.ds(h * SUB, SUB), :] + float(z_eigen[k])

    pstep_copy.wait_recv()
    step_copies = []
    for d in range(1, RING):
        _, target = along_ring(d)
        step_copies.append(send(
            pair_steps, all_steps.at[slot], step_send.at[d - 1], step_recv.at[d - 1], target
        ))
    all_steps[slot] = pair_steps[...]

    def table(i, carry):
        at = pl.ds(pl.multiple_of(i * 2 * SUB, 2 * SUB), 2 * SUB)
        for h in range(CHUNKS):
            for s in range(2):
                mu = pair_steps[s, 0:1, :] * lam[h, at, :]
                rho, square, v, left, a = responses(mu)
                tab[h, s, 0, at, :] = left
                tab[h, s, 1, at, :] = rho
                tab[h, s, 2, at, :] = a
                tab[h, s, 3, at, :] = square
                for n, m in enumerate((1, 3)):
                    w = [float(x) for x in INTERP[m]]
                    tab[h, s, 4 + 2 * n, at, :] = v[m] - w[0] + w[1] * (left - v[2]) + w[2] * (a - v[4])
                    tab[h, s, 5 + 2 * n, at, :] = w[0] + w[1] * rho + w[2] * square
        return carry

    lax.fori_loop(0, ROWS // (2 * SUB), table, 0)

    for copy in g_copies:
        copy.wait_recv()
    for s in (1, 0):
        for h in range(CHUNKS):
            planes = along_z([gin[s, z, pl.ds(h * SUB, SUB), :] for z in range(PLANES)], z_matrix)
            for k in range(PLANES):
                ghat[s, h, pl.ds(k * SUB, SUB), :] = planes[k]
        if s == 1:
            shift_copy = send(ghat.at[1], shifted, shift_sem.at[0], shift_sem.at[1], following)

    for copy in step_copies:
        copy.wait_recv()
    share = pl.ds(pl.multiple_of(slot * SUB, SUB), SUB)

    def pair_gain(i, carry):
        out = []
        for h in range(CHUNKS):
            total_g, total_a = carry[h]
            gains[i, 2, h] = total_g
            gains[i, 3, h] = total_a
            _, g0, _, _, a0 = responses(all_steps[i, 0, 0:1, :] * lam[h, share, :])
            _, g1, _, _, a1 = responses(all_steps[i, 1, 0:1, :] * lam[h, share, :])
            g, a = g1 * g0, g1 * a0 + a1 * g0
            gains[i, 0, h] = g
            gains[i, 1, h] = a
            out.append((g * total_g, g * total_a + a * total_g))
        return tuple(out)

    ones = jnp.ones((SUB, WIDTH), jnp.float32)
    zero = jnp.zeros((SUB, WIDTH), jnp.float32)
    ends = lax.fori_loop(0, RING, pair_gain, ((ones, zero),) * CHUNKS)
    for h in range(CHUNKS):
        gain_all[group, 0, h] = ends[h][0]
        gain_all[group, 1, h] = ends[h][1]
    gain_copies = [
        send(gain_all.at[group], gain_all.at[group], gain_send.at[d - 1], gain_recv.at[d - 1], across(d))
        for d in range(1, GROUPS)
    ]

    def pre(h):
        def step_pre(i, carry):
            two = pl.ds(pl.multiple_of(i * 2 * SUB, 2 * SUB), 2 * SUB)
            forced, extra = [], []
            for s in range(2):
                mu = pair_steps[s, 0:1, :] * lam[h, two, :]
                before = shifted[h, two, :] if s == 0 else ghat[0, h, two, :]
                f, v, left, b = sources([qhat[s, m, two, :] for m in range(4)], ghat[s, h, two, :], before, mu)
                alpha[h, s, 0, two, :] = left
                alpha[h, s, 1, two, :] = b
                for n, m in enumerate((1, 3)):
                    w = [float(x) for x in INTERP[m]]
                    alpha[h, s, 2 + n, two, :] = v[m] + w[1] * (left - v[2]) + w[2] * (b - v[4])
                if s == 0:
                    alpha[h, 0, 4, two, :] = f
                    begin = jnp.where(pair == 0, before, 0.0)
                    square, a = tab[h, 0, 3, two, :], tab[h, 0, 2, two, :]
                    f = f + square * begin
                    b = b + (square + a) * begin
                forced.append(f)
                extra.append(b)
            square, a = tab[h, 1, 3, two, :], tab[h, 1, 2, two, :]
            f = square * forced[0] + forced[1]
            b = square * extra[0] + (a * forced[0] + extra[1])
            for n in range(2):
                fb[h, 2 * i + n, 0] = f[n * SUB : (n + 1) * SUB]
                fb[h, 2 * i + n, 1] = b[n * SUB : (n + 1) * SUB]
            return carry

        lax.fori_loop(0, ROWS // (2 * SUB), step_pre, 0)

    scan_copies = []
    for h in range(CHUNKS):
        if h == 0:
            for copy in q_copies:
                copy.wait_recv()
        else:
            for copy in r_copies:
                copy.wait_recv()
        for s in range(2):
            for m in range(4):
                planes = along_z([qin[h, s, m, z] for z in range(PLANES)], z_matrix)
                for k in range(PLANES):
                    qhat[s, m, pl.ds(k * SUB, SUB), :] = planes[k]
        if h == 0:
            shift_copy.wait_recv()

            @pl.when(pair == 0)
            def _():
                for d in range(1, SPACES):
                    first_copy(d).wait_recv()
                for n in range(CHUNKS):
                    planes = along_z([firsts[z, pl.ds(n * SUB, SUB), :] for z in range(PLANES)], z_matrix)
                    for k in range(PLANES):
                        shifted[n, pl.ds(k * SUB, SUB), :] = planes[k]

        pre(h)
        for d in range(1, RING):
            other, target = along_ring(d)
            scan_copies.append(send(
                fb.at[h, other], scan_in.at[h, slot], scan_send.at[h, d - 1], scan_recv.at[h, d - 1], target
            ))
        scan_in[h, slot] = fb[h, slot]

    tot_copies = []
    for h in range(CHUNKS):
        for copy in scan_copies[h * (RING - 1) : (h + 1) * (RING - 1)]:
            copy.wait_recv()
        c, d = zero, zero
        for i in range(RING):
            f, b = scan_in[h, i, 0], scan_in[h, i, 1]
            back[h, i, 0] = c
            back[h, i, 1] = d
            g, a = gains[i, 0, h], gains[i, 1, h]
            c, d = g * c + f, g * d + (a * c + b)
        totals[h, group, 0] = c
        totals[h, group, 1] = d
        for n in range(1, GROUPS):
            tot_copies.append(send(
                totals.at[h, group], totals.at[h, group],
                tot_send.at[h, n - 1], tot_recv.at[h, n - 1], across(n),
            ))
    for copy in gain_copies:
        copy.wait_recv()
    back_copies = []
    for h in range(CHUNKS):
        for copy in tot_copies[h * (GROUPS - 1) : (h + 1) * (GROUPS - 1)]:
            copy.wait_recv()
        c, d = zero, zero
        start_c, start_d = zero, zero
        for other in range(GROUPS - 1):
            g, a = gain_all[other, 0, h], gain_all[other, 1, h]
            c, d = g * c + totals[h, other, 0], g * d + (a * c + totals[h, other, 1])
            start_c = jnp.where(group == other + 1, c, start_c)
            start_d = jnp.where(group == other + 1, d, start_d)
        for i in range(RING):
            g, a = gains[i, 2, h], gains[i, 3, h]
            back[h, i, 0] = back[h, i, 0] + g * start_c
            back[h, i, 1] = back[h, i, 1] + (g * start_d + a * start_c)
        for n in range(1, RING):
            other, target = along_ring(n)
            back_copies.append(send(
                back.at[h, other], cd.at[h, slot], back_send.at[h, n - 1], back_recv.at[h, n - 1], target
            ))
        cd[h, slot] = back[h, slot]

    order = (0, 4, 2, 1, 3)
    o_copies, m_copies = [], []
    for h in range(CHUNKS):
        for copy in back_copies[h * (RING - 1) : (h + 1) * (RING - 1)]:
            copy.wait_recv()
        for k in range(PLANES):
            at = pl.ds(k * SUB, SUB)
            before = shifted[h, at, :]
            c = jnp.where(pair == 0, before, cd[h, k, 0])
            d = jnp.where(pair == 0, before, cd[h, k, 1])
            g, a = tab[h, 0, 3, at, :], tab[h, 0, 2, at, :]
            cd[h, k, 0] = c
            cd[h, k, 1] = d
            cd_odd[h, k, 0] = g * c + alpha[h, 0, 4, at, :]
            cd_odd[h, k, 1] = g * d + (a * c + alpha[h, 0, 1, at, :])
        for m in order:
            for s in range(2):
                src = cd if s == 0 else cd_odd
                planes = []
                for k in range(PLANES):
                    at = pl.ds(k * SUB, SUB)
                    if m == 0:
                        planes.append(src[h, k, 1])
                    else:
                        n = {2: 0, 4: 1, 1: 2, 3: 3}[m]
                        planes.append(
                            alpha[h, s, n, at, :]
                            + (tab[h, s, 2 * n, at, :] * src[h, k, 0] + tab[h, s, 2 * n + 1, at, :] * src[h, k, 1])
                        )
                planes = along_z(planes, z_matrix)
                for z in range(PLANES):
                    yout[h, m, s, z] = planes[z]
            rows = yout[h, m].reshape(2 * ROWS, WIDTH)
            yout[h, m] = dot(rows, sin_ref[...]).reshape(2, PLANES, SUB, WIDTH)
            if h == CHUNKS - 1:
                for d in range(1, OWNERS):
                    other, target = owner(d)
                    m_copies.append(send(
                        yout.at[h, m, other // SPACES, pl.ds(lax.rem(other, SPACES) * DEPTH, DEPTH)],
                        outr.at[m, :, slab(own, h * SUB, SUB), :],
                        m_send.at[m, d - 1], m_recv.at[m, d - 1], target,
                    ))
            outr[m, :, slab(own, h * SUB, SUB), :] = yout[h, m, half, here]
        if h < CHUNKS - 1:
            for d in range(1, OWNERS):
                other, target = owner(d)
                o_copies.append(send(
                    yout.at[h, :, other // SPACES, pl.ds(lax.rem(other, SPACES) * DEPTH, DEPTH)],
                    outr.at[:, :, slab(own, h * SUB, SUB), :],
                    o_send.at[h, d - 1], o_recv.at[h, d - 1], target,
                ))

    for copy in o_copies:
        copy.wait_recv()
    for n, m in enumerate(order):
        for copy in m_copies[n * (OWNERS - 1) : (n + 1) * (OWNERS - 1)]:
            copy.wait_recv()
        for z in range(DEPTH):
            out_ref[0, m, z] = dot(sin_ref[...], outr[m, z])

    for copy in (
        [pstep_copy, shift_copy] + g_copies + q_copies + r_copies + step_copies + gain_copies
        + scan_copies + tot_copies + back_copies + o_copies + m_copies
    ):
        copy.wait_send()

    @pl.when(pair == 0)
    def _():
        for d in range(1, SPACES):
            first_copy(d).wait_send()


def body(initial, start_guess, forcing, step_size):
    table = jnp.asarray(sine(WIDTH), jnp.float32)
    lamxy = jnp.asarray(eigen(WIDTH)[:, None] + eigen(WIDTH)[None, :], jnp.float32)
    hbm = pl.BlockSpec(memory_space=pl.ANY)
    f32 = lambda *shape: pltpu.VMEM(shape, jnp.float32)
    dma = lambda *shape: pltpu.SemaphoreType.DMA(shape)
    tile = (SUB, WIDTH)
    return pl.pallas_call(
        kernel,
        out_shape=jax.ShapeDtypeStruct((1, 5, DEPTH, WIDTH, WIDTH), jnp.float32),
        in_specs=[hbm, hbm, hbm, pl.BlockSpec(memory_space=pltpu.SMEM), hbm, hbm],
        out_specs=pl.BlockSpec(memory_space=pltpu.VMEM),
        scratch_shapes=[
            f32(5, DEPTH, WIDTH, WIDTH), f32(DEPTH, WIDTH, WIDTH), f32(DEPTH, WIDTH, WIDTH),
            f32(WIDTH, WIDTH), f32(COLS, WIDTH), f32(6, DEPTH, WIDTH, WIDTH),
            f32(2, PLANES, COLS, WIDTH), f32(CHUNKS, 2, 4, PLANES, *tile), f32(PLANES, COLS, WIDTH),
            f32(2, CHUNKS, ROWS, WIDTH), f32(2, 4, ROWS, WIDTH), f32(CHUNKS, ROWS, WIDTH),
            f32(CHUNKS, ROWS, WIDTH), f32(CHUNKS, 2, 8, ROWS, WIDTH), f32(CHUNKS, 2, 5, ROWS, WIDTH),
            f32(2, *tile), f32(RING, 2, *tile), f32(RING, 4, CHUNKS, *tile), f32(GROUPS, 2, CHUNKS, *tile),
            f32(CHUNKS, RING, 2, *tile), f32(CHUNKS, RING, 2, *tile), f32(CHUNKS, GROUPS, 2, *tile),
            f32(CHUNKS, RING, 2, *tile), f32(CHUNKS, RING, 2, *tile), f32(CHUNKS, RING, 2, *tile),
            f32(CHUNKS, 5, 2, PLANES, *tile), f32(5, DEPTH, WIDTH, WIDTH),
            dma(5), dma(OWNERS - 1), dma(OWNERS - 1), dma(4, OWNERS - 1), dma(4, OWNERS - 1),
            dma(OWNERS - 1), dma(OWNERS - 1), dma(SPACES - 1), dma(SPACES - 1), dma(2),
            dma(2), dma(RING - 1), dma(RING - 1), dma(CHUNKS, RING - 1), dma(CHUNKS, RING - 1),
            dma(GROUPS - 1), dma(GROUPS - 1), dma(CHUNKS, GROUPS - 1), dma(CHUNKS, GROUPS - 1),
            dma(CHUNKS, RING - 1), dma(CHUNKS, RING - 1), dma(CHUNKS, OWNERS - 1), dma(CHUNKS, OWNERS - 1),
            dma(5, OWNERS - 1), dma(5, OWNERS - 1),
        ],
        compiler_params=pltpu.CompilerParams(collective_id=0, has_side_effects=True),
    )(start_guess, forcing, initial, step_size, table, lamxy)


def solution(mesh):
    placed = (
        P("space", None, None),
        P("tm", "space", None, None),
        P("tm", None, "space", None, None),
        P("tm"),
    )
    return jax.shard_map(
        body,
        mesh=mesh,
        in_specs=placed,
        out_specs=P("tm", None, "space", None, None),
        check_vma=False,
    )
```

time: 61 us -> 47.4 us (0.78)
  Pallas kernels: 58.2 us -> 44.6 us
    pallas_call x1, Pallas kernels: 58.2 us -> 44.6 us  [body(): pl.pallas_call(kernel, out_shape=jax.ShapeDtypeStruct((1, 5, DEPTH, WIDTH...]
where the time goes in v2:
time: 47.4 us; the launch traced here: 47.2 us
  Pallas kernels  44.6 us (94%)
  local copies, waits for them, and re-layouts  1.97 us (4%)
  between operations  0.66 us (1%)
    pallas_call x1, Pallas kernels, body(): pl.pallas_call(kernel, out_shape=jax.ShapeDtypeStruct((1, 5, DEPTH, WIDTH...  44.6 us
    unnamed x1, local copies, waits for them, and re-layouts  1.97 us

profile of v2, /device:TPU:1, one launch (start us, length us, event | category | flops | bytes accessed | tf_op | source)
XLA Modules:
  0.0 47.2 jit_solution(13701715538680864975)
XLA Ops:
  0.7 44.6 %shard_map.64 = f32[1,5,2,128,128]{4,3,2,1,0:T(8,128)} custom-call(f32[1,2,128,128]{3,2,1,0:T(8,128)} %start_hbm.1, f32[1,5,2,128,128]{4,3,2,1,0:T(8,128)} %force_hbm.1, f32[2,128,128]{2,1,0:T(8,128)} %first_hbm.1, f32[1]{0:T(128)S(6)} %copy.8.step_ref, f32[128,128]{1,0:T(8,128)} %constant.4.clone.sin_hbm, f32[128,128]{1,0:T(8,128)} %constant.5.clone.lamxy_hbm), custom_call_target="tpu_custom_call" | custom-call | tf_op jit(solution)/shard_map/pallas_call | solution.py:532
  45.3 2.0 %copy.9 = f32[1,5,2,128,128]{4,3,2,1,0:T(8,128)} copy(f32[1,5,2,128,128]{4,3,2,1,0:T(8,128)} %shard_map.64) | data formatting | bytes 1310720

commit v3 on v2

--- a/solution.py
+++ b/solution.py
@@ -21,6 +21,11 @@
 SUB = 8
 CHUNKS = COLS // SUB
 ROWS = PLANES * SUB
+
+GUESS, FIRST, SHIFT, PSTEP, STEPS, GAINS, OUT = range(7)
+FIELDS, SCAN, TOTALS, BACK = (7 + n * CHUNKS for n in range(4))
+LAST = 7 + 4 * CHUNKS
+PHASES = LAST + 5
 
 
 def node_tables():
@@ -137,21 +142,26 @@
 
 def kernel(
     start_hbm, force_hbm, first_hbm, step_ref, sin_hbm, lamxy_hbm, out_ref,
-    f_raw, g_raw, i_raw, sin_ref, lamxy, hat, gin, qin, firsts, ghat, qhat, shifted, lam, tab, alpha,
-    pair_steps, all_steps, gains, gain_all, fb, scan_in, totals, back, cd, cd_odd, yout, outr,
-    load_sem, g_send, g_recv, q_send, q_recv, r_send, r_recv, i_send, i_recv, shift_sem,
-    pstep_sem, step_send, step_recv, scan_send, scan_recv, gain_send, gain_recv, tot_send, tot_recv,
-    back_send, back_recv, o_send, o_recv, m_send, m_recv,
+    f_raw, g_raw, i_raw, sin_ref, lamxy, sin_hi, sin_lo, hat, gin, qin, firsts, ghat, qhat,
+    shifted, lam, tab, alpha, pair_steps, all_steps, gains, gain_all, fb, scan_in, totals, back, cd,
+    cd_odd, yout, outr, measure, load_sem, send_sem, recv_sem,
 ):
-    high = lax.Precision.HIGHEST
     tm = lax.axis_index("tm")
     sp = lax.axis_index("space")
     pair, half = tm // 2, tm % 2
     group, slot = pair // RING, pair % RING
     own = half * SPACES + sp
 
-    def dot(a, b):
-        return jnp.dot(a, b, precision=high, preferred_element_type=jnp.float32)
+    def halves(x):
+        hi = x.astype(jnp.bfloat16)
+        return hi, (x - hi.astype(jnp.float32)).astype(jnp.bfloat16)
+
+    def product(a, b):
+        dot = functools.partial(jnp.dot, preferred_element_type=jnp.float32)
+        return dot(a[0], b[0]) + (dot(a[0], b[1]) + dot(a[1], b[0]))
+
+    def matrix():
+        return sin_hi[...], sin_lo[...]
 
     def owner(d):
         other = lax.rem(own + d, OWNERS)
@@ -164,13 +174,27 @@
     def across(d):
         return ((lax.rem(group + d, GROUPS) * RING + slot) * 2 + half, sp)
 
-    def send(src, dst, send_sem, recv_sem, target):
-        copy = pltpu.make_async_remote_copy(
-            src_ref=src, dst_ref=dst, send_sem=send_sem, recv_sem=recv_sem,
+    sent = {}
+
+    def tiles(ref):
+        return math.prod(ref.shape) // (SUB * WIDTH)
+
+    def describe(src, dst, phase, target):
+        return pltpu.make_async_remote_copy(
+            src_ref=src, dst_ref=dst, send_sem=send_sem.at[phase], recv_sem=recv_sem.at[phase],
             device_id=target, device_id_type=MESH,
         )
-        copy.start()
-        return copy
+
+    def send(src, dst, phase, target):
+        describe(src, dst, phase, target).start()
+        sent[phase] = sent.get(phase, 0) + tiles(src)
+
+    def settle(sem, count):
+        some = measure.at[pl.ds(0, count)]
+        pltpu.make_async_copy(some, some, sem).wait()
+
+    def arrived(phase):
+        settle(recv_sem.at[phase], sent[phase])
 
     pairs = GROUPS * RING
     following = (lax.rem(pair + 1, pairs) * 2 + half, sp)
@@ -201,14 +225,16 @@
     greet(following)
     greet(preceding)
 
+    for load in loads[:2]:
+        load.wait()
     step = step_ref[0]
     pair_steps[half] = jnp.full((SUB, WIDTH), step, jnp.float32)
-    loads[0].wait()
-    loads[1].wait()
+    sin_hi[...], sin_lo[...] = halves(sin_ref[...])
 
     def transform(f, planes):
-        for z in range(DEPTH):
-            hat[f, z] = dot(dot(sin_ref[...], planes[z]), sin_ref[...])
+        wide = product(matrix(), halves(jnp.concatenate(planes, axis=1)))
+        tall = jnp.concatenate([wide[:, z * WIDTH : (z + 1) * WIDTH] for z in range(DEPTH)], axis=0)
+        hat[f] = product(halves(tall), matrix()).reshape(DEPTH, WIDTH, WIDTH)
 
     transform(4, [g_raw[z] for z in range(DEPTH)])
     loads[2].wait()
@@ -220,56 +246,37 @@
     def slab(other, first, size):
         return pl.ds(pl.multiple_of(other * COLS + first, SUB), size)
 
-    pstep_copy = send(
-        pair_steps.at[half], pair_steps.at[half], pstep_sem.at[0], pstep_sem.at[1], partner
-    )
-    g_copies = []
     for d in range(1, OWNERS):
         other, target = owner(d)
-        g_copies.append(send(
-            hat.at[4, :, slab(other, 0, COLS), :], gin.at[half, here],
-            g_send.at[d - 1], g_recv.at[d - 1], target,
-        ))
+        send(hat.at[4, :, slab(other, 0, COLS), :], gin.at[half, here], GUESS, target)
+    send(pair_steps.at[half], pair_steps.at[half], PSTEP, partner)
     gin[half, here] = hat[4, :, mine, :]
-    q_copies = []
     for m in range(4):
-        planes = [
+        transform(m, [
             step * mixed(QUAD[m], [f_raw[j, z] for j in range(5)]) for z in range(DEPTH)
-        ]
-        transform(m, planes)
+        ])
         for d in range(1, OWNERS):
             other, target = owner(d)
-            q_copies.append(send(
-                hat.at[m, :, slab(other, 0, SUB), :], qin.at[0, half, m, here],
-                q_send.at[m, d - 1], q_recv.at[m, d - 1], target,
-            ))
-    r_copies = []
+            send(hat.at[m, :, slab(other, 0, SUB), :], qin.at[0, half, m, here], FIELDS, target)
     for d in range(1, OWNERS):
         other, target = owner(d)
-        r_copies.append(send(
-            hat.at[pl.ds(0, 4), :, slab(other, SUB, SUB), :], qin.at[1, half, :, here],
-            r_send.at[d - 1], r_recv.at[d - 1], target,
-        ))
+        send(hat.at[pl.ds(0, 4), :, slab(other, SUB, SUB), :], qin.at[1, half, :, here], FIELDS + 1, target)
     for h in range(CHUNKS):
         for m in range(4):
             qin[h, half, m, here] = hat[m, :, slab(own, h * SUB, SUB), :]
 
     for load in loads[3:]:
         load.wait()
-
-    def first_copy(d):
-        other = lax.rem(sp + d, SPACES)
-        return pltpu.make_async_remote_copy(
-            src_ref=hat.at[5, :, slab(half * SPACES + other, 0, COLS), :],
-            dst_ref=firsts.at[here], send_sem=i_send.at[d - 1], recv_sem=i_recv.at[d - 1],
-            device_id=(tm, other), device_id_type=MESH,
-        )
+    first_tiles = (SPACES - 1) * DEPTH * COLS // SUB
 
     @pl.when(pair == 0)
     def _():
         transform(5, [i_raw[z] for z in range(DEPTH)])
         for d in range(1, SPACES):
-            first_copy(d).start()
+            other = lax.rem(sp + d, SPACES)
+            describe(
+                hat.at[5, :, slab(half * SPACES + other, 0, COLS), :], firsts.at[here], FIRST, (tm, other)
+            ).start()
         firsts[here] = hat[5, :, mine, :]
 
     z_matrix = sine(PLANES)
@@ -278,13 +285,9 @@
         for k in range(PLANES):
             lam[h, pl.ds(k * SUB, SUB), :] = lamxy[pl.ds(h * SUB, SUB), :] + float(z_eigen[k])
 
-    pstep_copy.wait_recv()
-    step_copies = []
+    arrived(PSTEP)
     for d in range(1, RING):
-        _, target = along_ring(d)
-        step_copies.append(send(
-            pair_steps, all_steps.at[slot], step_send.at[d - 1], step_recv.at[d - 1], target
-        ))
+        send(pair_steps, all_steps.at[slot], STEPS, along_ring(d)[1])
     all_steps[slot] = pair_steps[...]
 
     def table(i, carry):
@@ -305,44 +308,14 @@
 
     lax.fori_loop(0, ROWS // (2 * SUB), table, 0)
 
-    for copy in g_copies:
-        copy.wait_recv()
+    arrived(GUESS)
     for s in (1, 0):
         for h in range(CHUNKS):
             planes = along_z([gin[s, z, pl.ds(h * SUB, SUB), :] for z in range(PLANES)], z_matrix)
             for k in range(PLANES):
                 ghat[s, h, pl.ds(k * SUB, SUB), :] = planes[k]
         if s == 1:
-            shift_copy = send(ghat.at[1], shifted, shift_sem.at[0], shift_sem.at[1], following)
-
-    for copy in step_copies:
-        copy.wait_recv()
-    share = pl.ds(pl.multiple_of(slot * SUB, SUB), SUB)
-
-    def pair_gain(i, carry):
-        out = []
-        for h in range(CHUNKS):
-            total_g, total_a = carry[h]
-            gains[i, 2, h] = total_g
-            gains[i, 3, h] = total_a
-            _, g0, _, _, a0 = responses(all_steps[i, 0, 0:1, :] * lam[h, share, :])
-            _, g1, _, _, a1 = responses(all_steps[i, 1, 0:1, :] * lam[h, share, :])
-            g, a = g1 * g0, g1 * a0 + a1 * g0
-            gains[i, 0, h] = g
-            gains[i, 1, h] = a
-            out.append((g * total_g, g * total_a + a * total_g))
-        return tuple(out)
-
-    ones = jnp.ones((SUB, WIDTH), jnp.float32)
-    zero = jnp.zeros((SUB, WIDTH), jnp.float32)
-    ends = lax.fori_loop(0, RING, pair_gain, ((ones, zero),) * CHUNKS)
-    for h in range(CHUNKS):
-        gain_all[group, 0, h] = ends[h][0]
-        gain_all[group, 1, h] = ends[h][1]
-    gain_copies = [
-        send(gain_all.at[group], gain_all.at[group], gain_send.at[d - 1], gain_recv.at[d - 1], across(d))
-        for d in range(1, GROUPS)
-    ]
+            send(ghat.at[1], shifted, SHIFT, following)
 
     def pre(h):
         def step_pre(i, carry):
@@ -375,26 +348,19 @@
 
         lax.fori_loop(0, ROWS // (2 * SUB), step_pre, 0)
 
-    scan_copies = []
-    for h in range(CHUNKS):
-        if h == 0:
-            for copy in q_copies:
-                copy.wait_recv()
-        else:
-            for copy in r_copies:
-                copy.wait_recv()
+    for h in range(CHUNKS):
+        arrived(FIELDS + h)
         for s in range(2):
             for m in range(4):
                 planes = along_z([qin[h, s, m, z] for z in range(PLANES)], z_matrix)
                 for k in range(PLANES):
                     qhat[s, m, pl.ds(k * SUB, SUB), :] = planes[k]
         if h == 0:
-            shift_copy.wait_recv()
+            arrived(SHIFT)
 
             @pl.when(pair == 0)
             def _():
-                for d in range(1, SPACES):
-                    first_copy(d).wait_recv()
+                settle(recv_sem.at[FIRST], first_tiles)
                 for n in range(CHUNKS):
                     planes = along_z([firsts[z, pl.ds(n * SUB, SUB), :] for z in range(PLANES)], z_matrix)
                     for k in range(PLANES):
@@ -403,15 +369,37 @@
         pre(h)
         for d in range(1, RING):
             other, target = along_ring(d)
-            scan_copies.append(send(
-                fb.at[h, other], scan_in.at[h, slot], scan_send.at[h, d - 1], scan_recv.at[h, d - 1], target
-            ))
+            send(fb.at[h, other], scan_in.at[h, slot], SCAN + h, target)
         scan_in[h, slot] = fb[h, slot]
 
-    tot_copies = []
-    for h in range(CHUNKS):
-        for copy in scan_copies[h * (RING - 1) : (h + 1) * (RING - 1)]:
-            copy.wait_recv()
+    arrived(STEPS)
+    share = pl.ds(pl.multiple_of(slot * SUB, SUB), SUB)
+
+    def pair_gain(i, carry):
+        out = []
+        for h in range(CHUNKS):
+            total_g, total_a = carry[h]
+            gains[i, 2, h] = total_g
+            gains[i, 3, h] = total_a
+            _, g0, _, _, a0 = responses(all_steps[i, 0, 0:1, :] * lam[h, share, :])
+            _, g1, _, _, a1 = responses(all_steps[i, 1, 0:1, :] * lam[h, share, :])
+            g, a = g1 * g0, g1 * a0 + a1 * g0
+            gains[i, 0, h] = g
+            gains[i, 1, h] = a
+            out.append((g * total_g, g * total_a + a * total_g))
+        return tuple(out)
+
+    ones = jnp.ones((SUB, WIDTH), jnp.float32)
+    zero = jnp.zeros((SUB, WIDTH), jnp.float32)
+    ends = lax.fori_loop(0, RING, pair_gain, ((ones, zero),) * CHUNKS)
+    for h in range(CHUNKS):
+        gain_all[group, 0, h] = ends[h][0]
+        gain_all[group, 1, h] = ends[h][1]
+    for d in range(1, GROUPS):
+        send(gain_all.at[group], gain_all.at[group], GAINS, across(d))
+
+    for h in range(CHUNKS):
+        arrived(SCAN + h)
         c, d = zero, zero
         for i in range(RING):
             f, b = scan_in[h, i, 0], scan_in[h, i, 1]
@@ -422,16 +410,10 @@
         totals[h, group, 0] = c
         totals[h, group, 1] = d
         for n in range(1, GROUPS):
-            tot_copies.append(send(
-                totals.at[h, group], totals.at[h, group],
-                tot_send.at[h, n - 1], tot_recv.at[h, n - 1], across(n),
-            ))
-    for copy in gain_copies:
-        copy.wait_recv()
-    back_copies = []
-    for h in range(CHUNKS):
-        for copy in tot_copies[h * (GROUPS - 1) : (h + 1) * (GROUPS - 1)]:
-            copy.wait_recv()
+            send(totals.at[h, group], totals.at[h, group], TOTALS + h, across(n))
+    arrived(GAINS)
+    for h in range(CHUNKS):
+        arrived(TOTALS + h)
         c, d = zero, zero
         start_c, start_d = zero, zero
         for other in range(GROUPS - 1):
@@ -445,16 +427,12 @@
             back[h, i, 1] = back[h, i, 1] + (g * start_d + a * start_c)
         for n in range(1, RING):
             other, target = along_ring(n)
-            back_copies.append(send(
-                back.at[h, other], cd.at[h, slot], back_send.at[h, n - 1], back_recv.at[h, n - 1], target
-            ))
+            send(back.at[h, other], cd.at[h, slot], BACK + h, target)
         cd[h, slot] = back[h, slot]
 
     order = (0, 4, 2, 1, 3)
-    o_copies, m_copies = [], []
-    for h in range(CHUNKS):
-        for copy in back_copies[h * (RING - 1) : (h + 1) * (RING - 1)]:
-            copy.wait_recv()
+    for h in range(CHUNKS):
+        arrived(BACK + h)
         for k in range(PLANES):
             at = pl.ds(k * SUB, SUB)
             before = shifted[h, at, :]
@@ -466,6 +444,7 @@
             cd_odd[h, k, 0] = g * c + alpha[h, 0, 4, at, :]
             cd_odd[h, k, 1] = g * d + (a * c + alpha[h, 0, 1, at, :])
         for m in order:
+            rows = []
             for s in range(2):
                 src = cd if s == 0 else cd_odd
                 planes = []
@@ -479,56 +458,53 @@
                             alpha[h, s, n, at, :]
                             + (tab[h, s, 2 * n, at, :] * src[h, k, 0] + tab[h, s, 2 * n + 1, at, :] * src[h, k, 1])
                         )
-                planes = along_z(planes, z_matrix)
-                for z in range(PLANES):
-                    yout[h, m, s, z] = planes[z]
-            rows = yout[h, m].reshape(2 * ROWS, WIDTH)
-            yout[h, m] = dot(rows, sin_ref[...]).reshape(2, PLANES, SUB, WIDTH)
+                rows += along_z(planes, z_matrix)
+            rows = product(halves(jnp.concatenate(rows, axis=0)), matrix())
+            yout[h, m] = rows.reshape(2, PLANES, SUB, WIDTH)
             if h == CHUNKS - 1:
                 for d in range(1, OWNERS):
                     other, target = owner(d)
-                    m_copies.append(send(
+                    send(
                         yout.at[h, m, other // SPACES, pl.ds(lax.rem(other, SPACES) * DEPTH, DEPTH)],
-                        outr.at[m, :, slab(own, h * SUB, SUB), :],
-                        m_send.at[m, d - 1], m_recv.at[m, d - 1], target,
-                    ))
+                        outr.at[m, :, slab(own, h * SUB, SUB), :], LAST + m, target,
+                    )
             outr[m, :, slab(own, h * SUB, SUB), :] = yout[h, m, half, here]
         if h < CHUNKS - 1:
             for d in range(1, OWNERS):
                 other, target = owner(d)
-                o_copies.append(send(
+                send(
                     yout.at[h, :, other // SPACES, pl.ds(lax.rem(other, SPACES) * DEPTH, DEPTH)],
-                    outr.at[:, :, slab(own, h * SUB, SUB), :],
-                    o_send.at[h, d - 1], o_recv.at[h, d - 1], target,
-                ))
-
-    for copy in o_copies:
-        copy.wait_recv()
-    for n, m in enumerate(order):
-        for copy in m_copies[n * (OWNERS - 1) : (n + 1) * (OWNERS - 1)]:
-            copy.wait_recv()
+                    outr.at[:, :, slab(own, h * SUB, SUB), :], OUT, target,
+                )
+
+    arrived(OUT)
+    for m in order:
+        arrived(LAST + m)
+        wide = jnp.concatenate([outr[m, z] for z in range(DEPTH)], axis=1)
+        wide = product(matrix(), halves(wide))
         for z in range(DEPTH):
-            out_ref[0, m, z] = dot(sin_ref[...], outr[m, z])
-
-    for copy in (
-        [pstep_copy, shift_copy] + g_copies + q_copies + r_copies + step_copies + gain_copies
-        + scan_copies + tot_copies + back_copies + o_copies + m_copies
-    ):
-        copy.wait_send()
+            out_ref[0, m, z] = wide[:, z * WIDTH : (z + 1) * WIDTH]
+
+    for phase, count in sent.items():
+        settle(send_sem.at[phase], count)
 
     @pl.when(pair == 0)
     def _():
-        for d in range(1, SPACES):
-            first_copy(d).wait_send()
+        settle(send_sem.at[FIRST], first_tiles)
 
 
 def body(initial, start_guess, forcing, step_size):
     table = jnp.asarray(sine(WIDTH), jnp.float32)
     lamxy = jnp.asarray(eigen(WIDTH)[:, None] + eigen(WIDTH)[None, :], jnp.float32)
-    hbm = pl.BlockSpec(memory_space=pl.ANY)
+    hbm = pl.BlockSpec(memory_space=pltpu.HBM)
     f32 = lambda *shape: pltpu.VMEM(shape, jnp.float32)
     dma = lambda *shape: pltpu.SemaphoreType.DMA(shape)
     tile = (SUB, WIDTH)
+    bf16 = pltpu.VMEM((WIDTH, WIDTH), jnp.bfloat16)
+    start_guess, forcing, initial, table, lamxy = (
+        pltpu.with_memory_space_constraint(x, pltpu.HBM)
+        for x in (start_guess, forcing, initial, table, lamxy)
+    )
     return pl.pallas_call(
         kernel,
         out_shape=jax.ShapeDtypeStruct((1, 5, DEPTH, WIDTH, WIDTH), jnp.float32),
@@ -536,22 +512,20 @@
         out_specs=pl.BlockSpec(memory_space=pltpu.VMEM),
         scratch_shapes=[
             f32(5, DEPTH, WIDTH, WIDTH), f32(DEPTH, WIDTH, WIDTH), f32(DEPTH, WIDTH, WIDTH),
-            f32(WIDTH, WIDTH), f32(COLS, WIDTH), f32(6, DEPTH, WIDTH, WIDTH),
+            f32(WIDTH, WIDTH), f32(COLS, WIDTH), bf16, bf16,
+            f32(6, DEPTH, WIDTH, WIDTH),
             f32(2, PLANES, COLS, WIDTH), f32(CHUNKS, 2, 4, PLANES, *tile), f32(PLANES, COLS, WIDTH),
             f32(2, CHUNKS, ROWS, WIDTH), f32(2, 4, ROWS, WIDTH), f32(CHUNKS, ROWS, WIDTH),
             f32(CHUNKS, ROWS, WIDTH), f32(CHUNKS, 2, 8, ROWS, WIDTH), f32(CHUNKS, 2, 5, ROWS, WIDTH),
             f32(2, *tile), f32(RING, 2, *tile), f32(RING, 4, CHUNKS, *tile), f32(GROUPS, 2, CHUNKS, *tile),
             f32(CHUNKS, RING, 2, *tile), f32(CHUNKS, RING, 2, *tile), f32(CHUNKS, GROUPS, 2, *tile),
             f32(CHUNKS, RING, 2, *tile), f32(CHUNKS, RING, 2, *tile), f32(CHUNKS, RING, 2, *tile),
-            f32(CHUNKS, 5, 2, PLANES, *tile), f32(5, DEPTH, WIDTH, WIDTH),
-            dma(5), dma(OWNERS - 1), dma(OWNERS - 1), dma(4, OWNERS - 1), dma(4, OWNERS - 1),
-            dma(OWNERS - 1), dma(OWNERS - 1), dma(SPACES - 1), dma(SPACES - 1), dma(2),
-            dma(2), dma(RING - 1), dma(RING - 1), dma(CHUNKS, RING - 1), dma(CHUNKS, RING - 1),
-            dma(GROUPS - 1), dma(GROUPS - 1), dma(CHUNKS, GROUPS - 1), dma(CHUNKS, GROUPS - 1),
-            dma(CHUNKS, RING - 1), dma(CHUNKS, RING - 1), dma(CHUNKS, OWNERS - 1), dma(CHUNKS, OWNERS - 1),
-            dma(5, OWNERS - 1), dma(5, OWNERS - 1),
+            f32(CHUNKS, 5, 2, PLANES, *tile), f32(5, DEPTH, WIDTH, WIDTH), f32(80, *tile),
+            dma(5), dma(PHASES), dma(PHASES),
         ],
-        compiler_params=pltpu.CompilerParams(collective_id=0, has_side_effects=True),
+        compiler_params=pltpu.CompilerParams(
+            collective_id=0, has_side_effects=True, vmem_limit_bytes=16 * 1024 * 1024
+        ),
     )(start_guess, forcing, initial, step_size, table, lamxy)
 
 

time: 47.4 us -> 43.3 us (0.914)
  Pallas kernels: 44.6 us -> 41.7 us
  local copies, waits for them, and re-layouts: 1.97 us -> 0.84 us
    pallas_call x1, Pallas kernels: 44.6 us -> 41.7 us  [body(): pl.pallas_call(kernel, out_shape=jax.ShapeDtypeStruct((1, 5, DEPTH, WIDTH...]
    unnamed x1, local copies, waits for them, and re-layouts: 1.97 us -> 0.84 us
where the time goes in v3:
time: 43.3 us; the launch traced here: 43.2 us
  Pallas kernels  41.7 us (96%)
  local copies, waits for them, and re-layouts  0.84 us (2%)
  between operations  0.66 us (2%)
    pallas_call x1, Pallas kernels, body(): pl.pallas_call(kernel, out_shape=jax.ShapeDtypeStruct((1, 5, DEPTH, WIDTH...  41.7 us

profile of v3, /device:TPU:1, one launch (start us, length us, event | category | flops | bytes accessed | tf_op | source)
XLA Modules:
  0.0 43.2 jit_solution(1289445031956597949)
XLA Ops:
  0.7 41.7 %shard_map.64 = f32[1,5,2,128,128]{4,3,2,1,0:T(8,128)S(1)} custom-call(f32[1,2,128,128]{3,2,1,0:T(8,128)} %start_hbm.1, f32[1,5,2,128,128]{4,3,2,1,0:T(8,128)} %force_hbm.1, f32[2,128,128]{2,1,0:T(8,128)} %first_hbm.1, f32[1]{0:T(128)S(6)} %copy.8.step_ref, f32[128,128]{1,0:T(8,128)} %constant.4.clone.sin_hbm, f32[128,128]{1,0:T(8,128)} %constant.5.clone.lamxy_hbm), custom_call_target="tpu_custom_call" | custom-call | tf_op jit(solution)/shard_map/pallas_call | solution.py:508
  42.3 0.8 %copy.9 = f32[1,5,2,128,128]{4,3,2,1,0:T(8,128)} copy(f32[1,5,2,128,128]{4,3,2,1,0:T(8,128)S(1)} %shard_map.64) | data formatting | bytes 1310720

commit v4 on v3

--- a/solution.py
+++ b/solution.py
@@ -22,10 +22,13 @@
 CHUNKS = COLS // SUB
 ROWS = PLANES * SUB
 
-GUESS, FIRST, SHIFT, PSTEP, STEPS, GAINS, OUT = range(7)
-FIELDS, SCAN, TOTALS, BACK = (7 + n * CHUNKS for n in range(4))
-LAST = 7 + 4 * CHUNKS
-PHASES = LAST + 5
+OWNER_ORDER = (4, 3, 5, 2, 6, 1, 7)
+RING_ORDER = (4, 3, 5, 2, 6, 1, 7)
+GROUP_ORDER = (2, 1, 3)
+
+GUESS, FIRST, PSTEP, STEPS, GAINS, OUT, LAST = range(7)
+SHIFT, FIELDS, SCAN, TOTALS, BACK = (7 + n * CHUNKS for n in range(5))
+PHASES = 7 + 5 * CHUNKS
 
 
 def node_tables():
@@ -216,12 +219,12 @@
     def greet(target):
         pl.semaphore_signal(barrier, inc=1, device_id=target, device_id_type=MESH)
 
-    for d in range(1, OWNERS):
+    for d in RING_ORDER:
+        greet(along_ring(d)[1])
+    for d in GROUP_ORDER:
+        greet(across(d))
+    for d in OWNER_ORDER:
         greet(owner(d)[1])
-    for d in range(1, RING):
-        greet(along_ring(d)[1])
-    for d in range(1, GROUPS):
-        greet(across(d))
     greet(following)
     greet(preceding)
 
@@ -246,21 +249,18 @@
     def slab(other, first, size):
         return pl.ds(pl.multiple_of(other * COLS + first, SUB), size)
 
-    for d in range(1, OWNERS):
+    send(pair_steps.at[half], pair_steps.at[half], PSTEP, partner)
+    for d in OWNER_ORDER:
         other, target = owner(d)
         send(hat.at[4, :, slab(other, 0, COLS), :], gin.at[half, here], GUESS, target)
-    send(pair_steps.at[half], pair_steps.at[half], PSTEP, partner)
     gin[half, here] = hat[4, :, mine, :]
     for m in range(4):
         transform(m, [
             step * mixed(QUAD[m], [f_raw[j, z] for j in range(5)]) for z in range(DEPTH)
         ])
-        for d in range(1, OWNERS):
+        for d in OWNER_ORDER:
             other, target = owner(d)
             send(hat.at[m, :, slab(other, 0, SUB), :], qin.at[0, half, m, here], FIELDS, target)
-    for d in range(1, OWNERS):
-        other, target = owner(d)
-        send(hat.at[pl.ds(0, 4), :, slab(other, SUB, SUB), :], qin.at[1, half, :, here], FIELDS + 1, target)
     for h in range(CHUNKS):
         for m in range(4):
             qin[h, half, m, here] = hat[m, :, slab(own, h * SUB, SUB), :]
@@ -286,7 +286,7 @@
             lam[h, pl.ds(k * SUB, SUB), :] = lamxy[pl.ds(h * SUB, SUB), :] + float(z_eigen[k])
 
     arrived(PSTEP)
-    for d in range(1, RING):
+    for d in RING_ORDER:
         send(pair_steps, all_steps.at[slot], STEPS, along_ring(d)[1])
     all_steps[slot] = pair_steps[...]
 
@@ -314,8 +314,12 @@
             planes = along_z([gin[s, z, pl.ds(h * SUB, SUB), :] for z in range(PLANES)], z_matrix)
             for k in range(PLANES):
                 ghat[s, h, pl.ds(k * SUB, SUB), :] = planes[k]
-        if s == 1:
-            send(ghat.at[1], shifted, SHIFT, following)
+            if s == 1:
+                send(ghat.at[1, h], shifted.at[h], SHIFT + h, following)
+
+    for d in OWNER_ORDER:
+        other, target = owner(d)
+        send(hat.at[pl.ds(0, 4), :, slab(other, SUB, SUB), :], qin.at[1, half, :, here], FIELDS + 1, target)
 
     def pre(h):
         def step_pre(i, carry):
@@ -355,19 +359,18 @@
                 planes = along_z([qin[h, s, m, z] for z in range(PLANES)], z_matrix)
                 for k in range(PLANES):
                     qhat[s, m, pl.ds(k * SUB, SUB), :] = planes[k]
-        if h == 0:
-            arrived(SHIFT)
-
-            @pl.when(pair == 0)
-            def _():
+        arrived(SHIFT + h)
+
+        @pl.when(pair == 0)
+        def _():
+            if h == 0:
                 settle(recv_sem.at[FIRST], first_tiles)
-                for n in range(CHUNKS):
-                    planes = along_z([firsts[z, pl.ds(n * SUB, SUB), :] for z in range(PLANES)], z_matrix)
-                    for k in range(PLANES):
-                        shifted[n, pl.ds(k * SUB, SUB), :] = planes[k]
+            planes = along_z([firsts[z, pl.ds(h * SUB, SUB), :] for z in range(PLANES)], z_matrix)
+            for k in range(PLANES):
+                shifted[h, pl.ds(k * SUB, SUB), :] = planes[k]
 
         pre(h)
-        for d in range(1, RING):
+        for d in RING_ORDER:
             other, target = along_ring(d)
             send(fb.at[h, other], scan_in.at[h, slot], SCAN + h, target)
         scan_in[h, slot] = fb[h, slot]
@@ -395,7 +398,7 @@
     for h in range(CHUNKS):
         gain_all[group, 0, h] = ends[h][0]
         gain_all[group, 1, h] = ends[h][1]
-    for d in range(1, GROUPS):
+    for d in GROUP_ORDER:
         send(gain_all.at[group], gain_all.at[group], GAINS, across(d))
 
     for h in range(CHUNKS):
@@ -409,7 +412,7 @@
             c, d = g * c + f, g * d + (a * c + b)
         totals[h, group, 0] = c
         totals[h, group, 1] = d
-        for n in range(1, GROUPS):
+        for n in GROUP_ORDER:
             send(totals.at[h, group], totals.at[h, group], TOTALS + h, across(n))
     arrived(GAINS)
     for h in range(CHUNKS):
@@ -425,12 +428,11 @@
             g, a = gains[i, 2, h], gains[i, 3, h]
             back[h, i, 0] = back[h, i, 0] + g * start_c
             back[h, i, 1] = back[h, i, 1] + (g * start_d + a * start_c)
-        for n in range(1, RING):
+        for n in RING_ORDER:
             other, target = along_ring(n)
             send(back.at[h, other], cd.at[h, slot], BACK + h, target)
         cd[h, slot] = back[h, slot]
 
-    order = (0, 4, 2, 1, 3)
     for h in range(CHUNKS):
         arrived(BACK + h)
         for k in range(PLANES):
@@ -443,8 +445,8 @@
             cd[h, k, 1] = d
             cd_odd[h, k, 0] = g * c + alpha[h, 0, 4, at, :]
             cd_odd[h, k, 1] = g * d + (a * c + alpha[h, 0, 1, at, :])
-        for m in order:
-            rows = []
+        rows = []
+        for m in range(5):
             for s in range(2):
                 src = cd if s == 0 else cd_odd
                 planes = []
@@ -459,27 +461,19 @@
                             + (tab[h, s, 2 * n, at, :] * src[h, k, 0] + tab[h, s, 2 * n + 1, at, :] * src[h, k, 1])
                         )
                 rows += along_z(planes, z_matrix)
-            rows = product(halves(jnp.concatenate(rows, axis=0)), matrix())
-            yout[h, m] = rows.reshape(2, PLANES, SUB, WIDTH)
-            if h == CHUNKS - 1:
-                for d in range(1, OWNERS):
-                    other, target = owner(d)
-                    send(
-                        yout.at[h, m, other // SPACES, pl.ds(lax.rem(other, SPACES) * DEPTH, DEPTH)],
-                        outr.at[m, :, slab(own, h * SUB, SUB), :], LAST + m, target,
-                    )
-            outr[m, :, slab(own, h * SUB, SUB), :] = yout[h, m, half, here]
-        if h < CHUNKS - 1:
-            for d in range(1, OWNERS):
-                other, target = owner(d)
-                send(
-                    yout.at[h, :, other // SPACES, pl.ds(lax.rem(other, SPACES) * DEPTH, DEPTH)],
-                    outr.at[:, :, slab(own, h * SUB, SUB), :], OUT, target,
-                )
+        rows = product(halves(jnp.concatenate(rows, axis=0)), matrix())
+        yout[h] = rows.reshape(5, 2, PLANES, SUB, WIDTH)
+        for d in OWNER_ORDER:
+            other, target = owner(d)
+            send(
+                yout.at[h, :, other // SPACES, pl.ds(lax.rem(other, SPACES) * DEPTH, DEPTH)],
+                outr.at[:, :, slab(own, h * SUB, SUB), :], OUT if h < CHUNKS - 1 else LAST, target,
+            )
+        outr[:, :, slab(own, h * SUB, SUB), :] = yout[h, :, half, here]
 
     arrived(OUT)
-    for m in order:
-        arrived(LAST + m)
+    arrived(LAST)
+    for m in range(5):
         wide = jnp.concatenate([outr[m, z] for z in range(DEPTH)], axis=1)
         wide = product(matrix(), halves(wide))
         for z in range(DEPTH):

time: 43.3 us -> 41.7 us (0.963)
  Pallas kernels: 41.7 us -> 40.1 us
    pallas_call x1, Pallas kernels: 41.7 us -> 40.1 us  [body(): pl.pallas_call(kernel, out_shape=jax.ShapeDtypeStruct((1, 5, DEPTH, WIDTH...]
where the time goes in v4:
time: 41.7 us; the launch traced here: 41.6 us
  Pallas kernels  40.1 us (96%)
  local copies, waits for them, and re-layouts  0.84 us (2%)
  between operations  0.66 us (2%)
    pallas_call x1, Pallas kernels, body(): pl.pallas_call(kernel, out_shape=jax.ShapeDtypeStruct((1, 5, DEPTH, WIDTH...  40.1 us
    unnamed x1, local copies, waits for them, and re-layouts  0.84 us

profile of v4, /device:TPU:1, one launch (start us, length us, event | category | flops | bytes accessed | tf_op | source)
XLA Modules:
  0.0 41.6 jit_solution(4419515807358482231)
XLA Ops:
  0.7 40.1 %shard_map.64 = f32[1,5,2,128,128]{4,3,2,1,0:T(8,128)S(1)} custom-call(f32[1,2,128,128]{3,2,1,0:T(8,128)} %start_hbm.1, f32[1,5,2,128,128]{4,3,2,1,0:T(8,128)} %force_hbm.1, f32[2,128,128]{2,1,0:T(8,128)} %first_hbm.1, f32[1]{0:T(128)S(6)} %copy.8.step_ref, f32[128,128]{1,0:T(8,128)} %constant.4.clone.sin_hbm, f32[128,128]{1,0:T(8,128)} %constant.5.clone.lamxy_hbm), custom_call_target="tpu_custom_call" | custom-call | tf_op jit(solution)/shard_map/pallas_call | solution.py:502
  40.8 0.8 %copy.9 = f32[1,5,2,128,128]{4,3,2,1,0:T(8,128)} copy(f32[1,5,2,128,128]{4,3,2,1,0:T(8,128)S(1)} %shard_map.64) | data formatting | bytes 1310720

commit v5 on v4

--- a/solution.py
+++ b/solution.py
@@ -19,16 +19,16 @@
 WIDTH = 128
 COLS = WIDTH // OWNERS
 SUB = 8
-CHUNKS = COLS // SUB
-ROWS = PLANES * SUB
+SPLIT = SUB // 2
+CHUNKS = COLS // SPLIT
 
 OWNER_ORDER = (4, 3, 5, 2, 6, 1, 7)
 RING_ORDER = (4, 3, 5, 2, 6, 1, 7)
 GROUP_ORDER = (2, 1, 3)
 
-GUESS, FIRST, PSTEP, STEPS, GAINS, OUT, LAST = range(7)
-SHIFT, FIELDS, SCAN, TOTALS, BACK = (7 + n * CHUNKS for n in range(5))
-PHASES = 7 + 5 * CHUNKS
+GUESS, FIRST, PSTEP, STEPS, GAINS, SHIFT = range(6)
+FIELDS, SCAN, TOTALS, BACK, OUT = (8 + n * CHUNKS for n in range(5))
+PHASES = 8 + 5 * CHUNKS
 
 
 def node_tables():
@@ -145,9 +145,9 @@
 
 def kernel(
     start_hbm, force_hbm, first_hbm, step_ref, sin_hbm, lamxy_hbm, out_ref,
-    f_raw, g_raw, i_raw, sin_ref, lamxy, sin_hi, sin_lo, hat, gin, qin, firsts, ghat, qhat,
-    shifted, lam, tab, alpha, pair_steps, all_steps, gains, gain_all, fb, scan_in, totals, back, cd,
-    cd_odd, yout, outr, measure, load_sem, send_sem, recv_sem,
+    f_raw, g_raw, i_raw, sin_ref, lamxy, sin_hi, sin_lo, hat, gin, qin, firsts, ghat, shifted, guess,
+    earlier, qhat, lam, tab, alpha, pair_steps, step_tile, all_steps, gains, gain_all, fb, scan_in,
+    totals, partial, back, cd, starts, yout, outr, measure, load_sem, send_sem, recv_sem, local_sem,
 ):
     tm = lax.axis_index("tm")
     sp = lax.axis_index("space")
@@ -179,9 +179,6 @@
 
     sent = {}
 
-    def tiles(ref):
-        return math.prod(ref.shape) // (SUB * WIDTH)
-
     def describe(src, dst, phase, target):
         return pltpu.make_async_remote_copy(
             src_ref=src, dst_ref=dst, send_sem=send_sem.at[phase], recv_sem=recv_sem.at[phase],
@@ -190,10 +187,10 @@
 
     def send(src, dst, phase, target):
         describe(src, dst, phase, target).start()
-        sent[phase] = sent.get(phase, 0) + tiles(src)
+        sent[phase] = sent.get(phase, 0) + math.prod(src.shape)
 
     def settle(sem, count):
-        some = measure.at[pl.ds(0, count)]
+        some = measure.at[pl.ds(0, count // (SUB * WIDTH))]
         pltpu.make_async_copy(some, some, sem).wait()
 
     def arrived(phase):
@@ -245,9 +242,17 @@
 
     mine = pl.ds(pl.multiple_of(own * COLS, COLS), COLS)
     here = pl.ds(sp * DEPTH, DEPTH)
+    part = pl.ds(pl.multiple_of(half * SPLIT, SPLIT), SPLIT)
 
     def slab(other, first, size):
-        return pl.ds(pl.multiple_of(other * COLS + first, SUB), size)
+        return pl.ds(pl.multiple_of(other * COLS + first, SPLIT), size)
+
+    def swap(x):
+        return pltpu.roll(x, SPLIT, x.ndim - 2)
+
+    def pick(upper, lower):
+        row = lax.broadcasted_iota(jnp.int32, (SUB, WIDTH), 0)
+        return jnp.where(row < SPLIT, upper, lower)
 
     send(pair_steps.at[half], pair_steps.at[half], PSTEP, partner)
     for d in OWNER_ORDER:
@@ -260,14 +265,19 @@
         ])
         for d in OWNER_ORDER:
             other, target = owner(d)
-            send(hat.at[m, :, slab(other, 0, SUB), :], qin.at[0, half, m, here], FIELDS, target)
-    for h in range(CHUNKS):
-        for m in range(4):
-            qin[h, half, m, here] = hat[m, :, slab(own, h * SUB, SUB), :]
+            send(hat.at[m, :, slab(other, 0, SPLIT), :], qin.at[0, m, here, part, :], FIELDS, target)
+    kept = [
+        pltpu.make_async_copy(
+            hat.at[pl.ds(0, 4), :, slab(own, h * SPLIT, SPLIT), :], qin.at[h, :, here, part, :], local_sem.at[h]
+        )
+        for h in range(CHUNKS)
+    ]
+    for copy in kept:
+        copy.start()
 
     for load in loads[3:]:
         load.wait()
-    first_tiles = (SPACES - 1) * DEPTH * COLS // SUB
+    first_size = (SPACES - 1) * DEPTH * COLS * WIDTH
 
     @pl.when(pair == 0)
     def _():
@@ -279,96 +289,113 @@
             ).start()
         firsts[here] = hat[5, :, mine, :]
 
+    def send_fields(h):
+        for d in OWNER_ORDER:
+            other, target = owner(d)
+            send(
+                hat.at[pl.ds(0, 4), :, slab(other, h * SPLIT, SPLIT), :], qin.at[h, :, here, part, :],
+                FIELDS + h, target,
+            )
+
     z_matrix = sine(PLANES)
     z_eigen = eigen(PLANES)
     for h in range(CHUNKS):
+        both = lamxy[pl.ds(h // 2 * SUB, SUB), :]
+        both = pick(both, swap(both)) if h % 2 == 0 else pick(swap(both), both)
         for k in range(PLANES):
-            lam[h, pl.ds(k * SUB, SUB), :] = lamxy[pl.ds(h * SUB, SUB), :] + float(z_eigen[k])
+            lam[h, k] = both + float(z_eigen[k])
 
     arrived(PSTEP)
+    step_tile[...] = pick(pair_steps[0], pair_steps[1])
     for d in RING_ORDER:
-        send(pair_steps, all_steps.at[slot], STEPS, along_ring(d)[1])
-    all_steps[slot] = pair_steps[...]
+        send(step_tile, all_steps.at[slot], STEPS, along_ring(d)[1])
+    all_steps[slot] = step_tile[...]
 
     def table(i, carry):
-        at = pl.ds(pl.multiple_of(i * 2 * SUB, 2 * SUB), 2 * SUB)
+        two = pl.ds(i * 2, 2)
         for h in range(CHUNKS):
-            for s in range(2):
-                mu = pair_steps[s, 0:1, :] * lam[h, at, :]
-                rho, square, v, left, a = responses(mu)
-                tab[h, s, 0, at, :] = left
-                tab[h, s, 1, at, :] = rho
-                tab[h, s, 2, at, :] = a
-                tab[h, s, 3, at, :] = square
-                for n, m in enumerate((1, 3)):
-                    w = [float(x) for x in INTERP[m]]
-                    tab[h, s, 4 + 2 * n, at, :] = v[m] - w[0] + w[1] * (left - v[2]) + w[2] * (a - v[4])
-                    tab[h, s, 5 + 2 * n, at, :] = w[0] + w[1] * rho + w[2] * square
+            mu = step_tile[...] * lam[h, two]
+            rho, square, v, left, a = responses(mu)
+            tab[h, 0, two] = left
+            tab[h, 1, two] = rho
+            tab[h, 2, two] = a
+            tab[h, 3, two] = square
+            for n, m in enumerate((1, 3)):
+                w = [float(x) for x in INTERP[m]]
+                tab[h, 4 + 2 * n, two] = v[m] - w[0] + w[1] * (left - v[2]) + w[2] * (a - v[4])
+                tab[h, 5 + 2 * n, two] = w[0] + w[1] * rho + w[2] * square
+            tab[h, 8, two] = pick(1.0, swap(square))
+            tab[h, 9, two] = pick(0.0, swap(a))
         return carry
 
-    lax.fori_loop(0, ROWS // (2 * SUB), table, 0)
+    lax.fori_loop(0, PLANES // 2, table, 0)
+    send_fields(1)
 
     arrived(GUESS)
     for s in (1, 0):
-        for h in range(CHUNKS):
-            planes = along_z([gin[s, z, pl.ds(h * SUB, SUB), :] for z in range(PLANES)], z_matrix)
+        for n in range(COLS // SUB):
+            planes = along_z([gin[s, z, pl.ds(n * SUB, SUB), :] for z in range(PLANES)], z_matrix)
             for k in range(PLANES):
-                ghat[s, h, pl.ds(k * SUB, SUB), :] = planes[k]
+                ghat[s, n, k] = planes[k]
             if s == 1:
-                send(ghat.at[1, h], shifted.at[h], SHIFT + h, following)
-
-    for d in OWNER_ORDER:
-        other, target = owner(d)
-        send(hat.at[pl.ds(0, 4), :, slab(other, SUB, SUB), :], qin.at[1, half, :, here], FIELDS + 1, target)
+                send(ghat.at[1, n], shifted.at[n], SHIFT + n, following)
+    for h in range(2, CHUNKS):
+        send_fields(h)
+    for h in range(CHUNKS):
+        for k in range(PLANES):
+            upper, lower = ghat[0, h // 2, k], ghat[1, h // 2, k]
+            guess[h, k] = pick(upper, swap(lower)) if h % 2 == 0 else pick(swap(upper), lower)
+
+    opening = pick(jnp.where(pair == 0, 1.0, 0.0), 0.0)
 
     def pre(h):
         def step_pre(i, carry):
-            two = pl.ds(pl.multiple_of(i * 2 * SUB, 2 * SUB), 2 * SUB)
-            forced, extra = [], []
-            for s in range(2):
-                mu = pair_steps[s, 0:1, :] * lam[h, two, :]
-                before = shifted[h, two, :] if s == 0 else ghat[0, h, two, :]
-                f, v, left, b = sources([qhat[s, m, two, :] for m in range(4)], ghat[s, h, two, :], before, mu)
-                alpha[h, s, 0, two, :] = left
-                alpha[h, s, 1, two, :] = b
-                for n, m in enumerate((1, 3)):
-                    w = [float(x) for x in INTERP[m]]
-                    alpha[h, s, 2 + n, two, :] = v[m] + w[1] * (left - v[2]) + w[2] * (b - v[4])
-                if s == 0:
-                    alpha[h, 0, 4, two, :] = f
-                    begin = jnp.where(pair == 0, before, 0.0)
-                    square, a = tab[h, 0, 3, two, :], tab[h, 0, 2, two, :]
-                    f = f + square * begin
-                    b = b + (square + a) * begin
-                forced.append(f)
-                extra.append(b)
-            square, a = tab[h, 1, 3, two, :], tab[h, 1, 2, two, :]
-            f = square * forced[0] + forced[1]
-            b = square * extra[0] + (a * forced[0] + extra[1])
-            for n in range(2):
-                fb[h, 2 * i + n, 0] = f[n * SUB : (n + 1) * SUB]
-                fb[h, 2 * i + n, 1] = b[n * SUB : (n + 1) * SUB]
+            two = pl.ds(i * 2, 2)
+            mu = step_tile[...] * lam[h, two]
+            before = earlier[h, two]
+            f, v, left, b = sources([qhat[m, two] for m in range(4)], guess[h, two], before, mu)
+            alpha[h, 0, two] = left
+            alpha[h, 1, two] = b
+            for n, m in enumerate((1, 3)):
+                w = [float(x) for x in INTERP[m]]
+                alpha[h, 2 + n, two] = v[m] + w[1] * (left - v[2]) + w[2] * (b - v[4])
+            alpha[h, 4, two] = pick(0.0, swap(f))
+            alpha[h, 5, two] = pick(0.0, swap(b))
+            begin = before * opening
+            square, a = tab[h, 3, two], tab[h, 2, two]
+            f = f + square * begin
+            b = b + (square + a) * begin
+            first_f, first_b = swap(f), swap(b)
+            pair_f = square * first_f + f
+            pair_b = square * first_b + (a * first_f + b)
+            fb[h, two] = pick(swap(pair_f), pair_b)
             return carry
 
-        lax.fori_loop(0, ROWS // (2 * SUB), step_pre, 0)
+        lax.fori_loop(0, PLANES // 2, step_pre, 0)
 
     for h in range(CHUNKS):
+        kept[h].wait()
         arrived(FIELDS + h)
-        for s in range(2):
-            for m in range(4):
-                planes = along_z([qin[h, s, m, z] for z in range(PLANES)], z_matrix)
+        for m in range(4):
+            planes = along_z([qin[h, m, z] for z in range(PLANES)], z_matrix)
+            for k in range(PLANES):
+                qhat[m, k] = planes[k]
+        if h % 2 == 0:
+            n = h // 2
+            arrived(SHIFT + n)
+
+            @pl.when(pair == 0)
+            def _():
+                if h == 0:
+                    settle(recv_sem.at[FIRST], first_size)
+                planes = along_z([firsts[z, pl.ds(n * SUB, SUB), :] for z in range(PLANES)], z_matrix)
                 for k in range(PLANES):
-                    qhat[s, m, pl.ds(k * SUB, SUB), :] = planes[k]
-        arrived(SHIFT + h)
-
-        @pl.when(pair == 0)
-        def _():
-            if h == 0:
-                settle(recv_sem.at[FIRST], first_tiles)
-            planes = along_z([firsts[z, pl.ds(h * SUB, SUB), :] for z in range(PLANES)], z_matrix)
+                    shifted[n, k] = planes[k]
+
             for k in range(PLANES):
-                shifted[h, pl.ds(k * SUB, SUB), :] = planes[k]
-
+                upper, lower = shifted[n, k], ghat[0, n, k]
+                earlier[h, k] = pick(upper, swap(lower))
+                earlier[h + 1, k] = pick(swap(upper), lower)
         pre(h)
         for d in RING_ORDER:
             other, target = along_ring(d)
@@ -376,7 +403,6 @@
         scan_in[h, slot] = fb[h, slot]
 
     arrived(STEPS)
-    share = pl.ds(pl.multiple_of(slot * SUB, SUB), SUB)
 
     def pair_gain(i, carry):
         out = []
@@ -384,9 +410,11 @@
             total_g, total_a = carry[h]
             gains[i, 2, h] = total_g
             gains[i, 3, h] = total_a
-            _, g0, _, _, a0 = responses(all_steps[i, 0, 0:1, :] * lam[h, share, :])
-            _, g1, _, _, a1 = responses(all_steps[i, 1, 0:1, :] * lam[h, share, :])
-            g, a = g1 * g0, g1 * a0 + a1 * g0
+            _, square, _, _, a = responses(all_steps[i] * lam[h, slot])
+            other = swap(square)
+            g = square * other
+            a = other * a
+            a = a + swap(a)
             gains[i, 0, h] = g
             gains[i, 1, h] = a
             out.append((g * total_g, g * total_a + a * total_g))
@@ -401,78 +429,102 @@
     for d in GROUP_ORDER:
         send(gain_all.at[group], gain_all.at[group], GAINS, across(d))
 
-    for h in range(CHUNKS):
+    def advance(h):
         arrived(SCAN + h)
         c, d = zero, zero
         for i in range(RING):
-            f, b = scan_in[h, i, 0], scan_in[h, i, 1]
-            back[h, i, 0] = c
-            back[h, i, 1] = d
+            f = scan_in[h, i]
+            b = swap(f)
+            partial[h, i, 0] = c
+            partial[h, i, 1] = d
             g, a = gains[i, 0, h], gains[i, 1, h]
             c, d = g * c + f, g * d + (a * c + b)
-        totals[h, group, 0] = c
-        totals[h, group, 1] = d
+        totals[h, group] = pick(c, swap(d))
         for n in GROUP_ORDER:
             send(totals.at[h, group], totals.at[h, group], TOTALS + h, across(n))
-    arrived(GAINS)
-    for h in range(CHUNKS):
+
+    def fold(h):
+        if h == 0:
+            arrived(GAINS)
         arrived(TOTALS + h)
         c, d = zero, zero
         start_c, start_d = zero, zero
         for other in range(GROUPS - 1):
             g, a = gain_all[other, 0, h], gain_all[other, 1, h]
-            c, d = g * c + totals[h, other, 0], g * d + (a * c + totals[h, other, 1])
+            f = totals[h, other]
+            c, d = g * c + f, g * d + (a * c + swap(f))
             start_c = jnp.where(group == other + 1, c, start_c)
             start_d = jnp.where(group == other + 1, d, start_d)
         for i in range(RING):
             g, a = gains[i, 2, h], gains[i, 3, h]
-            back[h, i, 0] = back[h, i, 0] + g * start_c
-            back[h, i, 1] = back[h, i, 1] + (g * start_d + a * start_c)
+            c = partial[h, i, 0] + g * start_c
+            d = partial[h, i, 1] + (g * start_d + a * start_c)
+            back[h, i] = pick(c, swap(d))
         for n in RING_ORDER:
             other, target = along_ring(n)
             send(back.at[h, other], cd.at[h, slot], BACK + h, target)
         cd[h, slot] = back[h, slot]
 
-    for h in range(CHUNKS):
+    returned = []
+
+    def give(h):
         arrived(BACK + h)
+
+        @pl.when(pair == 0)
+        def _():
+            for k in range(PLANES):
+                before = earlier[h, k]
+                cd[h, k] = pick(before, swap(before))
+
         for k in range(PLANES):
-            at = pl.ds(k * SUB, SUB)
-            before = shifted[h, at, :]
-            c = jnp.where(pair == 0, before, cd[h, k, 0])
-            d = jnp.where(pair == 0, before, cd[h, k, 1])
-            g, a = tab[h, 0, 3, at, :], tab[h, 0, 2, at, :]
-            cd[h, k, 0] = c
-            cd[h, k, 1] = d
-            cd_odd[h, k, 0] = g * c + alpha[h, 0, 4, at, :]
-            cd_odd[h, k, 1] = g * d + (a * c + alpha[h, 0, 1, at, :])
+            tile = cd[h, k]
+            turned = swap(tile)
+            c, d = pick(tile, turned), pick(turned, tile)
+            starts[0, k] = tab[h, 8, k] * c + alpha[h, 4, k]
+            starts[1, k] = tab[h, 8, k] * d + (tab[h, 9, k] * c + alpha[h, 5, k])
         rows = []
         for m in range(5):
-            for s in range(2):
-                src = cd if s == 0 else cd_odd
-                planes = []
-                for k in range(PLANES):
-                    at = pl.ds(k * SUB, SUB)
-                    if m == 0:
-                        planes.append(src[h, k, 1])
-                    else:
-                        n = {2: 0, 4: 1, 1: 2, 3: 3}[m]
-                        planes.append(
-                            alpha[h, s, n, at, :]
-                            + (tab[h, s, 2 * n, at, :] * src[h, k, 0] + tab[h, s, 2 * n + 1, at, :] * src[h, k, 1])
-                        )
-                rows += along_z(planes, z_matrix)
+            planes = []
+            for k in range(PLANES):
+                if m == 0:
+                    planes.append(starts[1, k])
+                else:
+                    n = {2: 0, 4: 1, 1: 2, 3: 3}[m]
+                    planes.append(
+                        alpha[h, n, k] + (tab[h, 2 * n, k] * starts[0, k] + tab[h, 2 * n + 1, k] * starts[1, k])
+                    )
+            rows += along_z(planes, z_matrix)
         rows = product(halves(jnp.concatenate(rows, axis=0)), matrix())
-        yout[h] = rows.reshape(5, 2, PLANES, SUB, WIDTH)
+        yout[h] = rows.reshape(5, PLANES, SUB, WIDTH)
         for d in OWNER_ORDER:
             other, target = owner(d)
+            rows = pl.ds(pl.multiple_of(other // SPACES * SPLIT, SPLIT), SPLIT)
             send(
-                yout.at[h, :, other // SPACES, pl.ds(lax.rem(other, SPACES) * DEPTH, DEPTH)],
-                outr.at[:, :, slab(own, h * SUB, SUB), :], OUT if h < CHUNKS - 1 else LAST, target,
+                yout.at[h, :, pl.ds(lax.rem(other, SPACES) * DEPTH, DEPTH), rows, :],
+                outr.at[:, :, slab(own, h * SPLIT, SPLIT), :], OUT + h, target,
             )
-        outr[:, :, slab(own, h * SUB, SUB), :] = yout[h, :, half, here]
-
-    arrived(OUT)
-    arrived(LAST)
+        copy = pltpu.make_async_copy(
+            yout.at[h, :, here, part, :], outr.at[:, :, slab(own, h * SPLIT, SPLIT), :], local_sem.at[CHUNKS + h]
+        )
+        copy.start()
+        returned.append(copy)
+
+    advance(0)
+    advance(1)
+    advance(2)
+    fold(0)
+    fold(1)
+    advance(3)
+    fold(2)
+    give(0)
+    fold(3)
+    give(1)
+    give(2)
+    give(3)
+
+    for h in range(CHUNKS):
+        returned[h].wait()
+        arrived(OUT + h)
     for m in range(5):
         wide = jnp.concatenate([outr[m, z] for z in range(DEPTH)], axis=1)
         wide = product(matrix(), halves(wide))
@@ -484,7 +536,7 @@
 
     @pl.when(pair == 0)
     def _():
-        settle(send_sem.at[FIRST], first_tiles)
+        settle(send_sem.at[FIRST], first_size)
 
 
 def body(initial, start_guess, forcing, step_size):
@@ -506,16 +558,16 @@
         out_specs=pl.BlockSpec(memory_space=pltpu.VMEM),
         scratch_shapes=[
             f32(5, DEPTH, WIDTH, WIDTH), f32(DEPTH, WIDTH, WIDTH), f32(DEPTH, WIDTH, WIDTH),
-            f32(WIDTH, WIDTH), f32(COLS, WIDTH), bf16, bf16,
-            f32(6, DEPTH, WIDTH, WIDTH),
-            f32(2, PLANES, COLS, WIDTH), f32(CHUNKS, 2, 4, PLANES, *tile), f32(PLANES, COLS, WIDTH),
-            f32(2, CHUNKS, ROWS, WIDTH), f32(2, 4, ROWS, WIDTH), f32(CHUNKS, ROWS, WIDTH),
-            f32(CHUNKS, ROWS, WIDTH), f32(CHUNKS, 2, 8, ROWS, WIDTH), f32(CHUNKS, 2, 5, ROWS, WIDTH),
-            f32(2, *tile), f32(RING, 2, *tile), f32(RING, 4, CHUNKS, *tile), f32(GROUPS, 2, CHUNKS, *tile),
-            f32(CHUNKS, RING, 2, *tile), f32(CHUNKS, RING, 2, *tile), f32(CHUNKS, GROUPS, 2, *tile),
-            f32(CHUNKS, RING, 2, *tile), f32(CHUNKS, RING, 2, *tile), f32(CHUNKS, RING, 2, *tile),
-            f32(CHUNKS, 5, 2, PLANES, *tile), f32(5, DEPTH, WIDTH, WIDTH), f32(80, *tile),
-            dma(5), dma(PHASES), dma(PHASES),
+            f32(WIDTH, WIDTH), f32(COLS, WIDTH), bf16, bf16, f32(6, DEPTH, WIDTH, WIDTH),
+            f32(2, PLANES, COLS, WIDTH), f32(CHUNKS, 4, PLANES, *tile), f32(PLANES, COLS, WIDTH),
+            f32(2, COLS // SUB, PLANES, *tile), f32(COLS // SUB, PLANES, *tile), f32(CHUNKS, PLANES, *tile),
+            f32(CHUNKS, PLANES, *tile), f32(4, PLANES, *tile), f32(CHUNKS, PLANES, *tile),
+            f32(CHUNKS, 10, PLANES, *tile), f32(CHUNKS, 6, PLANES, *tile), f32(2, *tile), f32(*tile),
+            f32(RING, *tile), f32(RING, 4, CHUNKS, *tile), f32(GROUPS, 2, CHUNKS, *tile),
+            f32(CHUNKS, RING, *tile), f32(CHUNKS, RING, *tile), f32(CHUNKS, GROUPS, *tile),
+            f32(CHUNKS, RING, 2, *tile), f32(CHUNKS, RING, *tile), f32(CHUNKS, RING, *tile),
+            f32(2, PLANES, *tile), f32(CHUNKS, 5, PLANES, *tile), f32(5, DEPTH, WIDTH, WIDTH), f32(80, *tile),
+            dma(5), dma(PHASES), dma(PHASES), dma(2 * CHUNKS),
         ],
         compiler_params=pltpu.CompilerParams(
             collective_id=0, has_side_effects=True, vmem_limit_bytes=16 * 1024 * 1024

time: 41.7 us -> 43 us (1.031)
  Pallas kernels: 40.1 us -> 41.4 us
    pallas_call x1, Pallas kernels: 40.1 us -> 41.4 us  [body(): pl.pallas_call(kernel, out_shape=jax.ShapeDtypeStruct((1, 5, DEPTH, WIDTH...]
where the time goes in v5:
time: 43 us; the launch traced here: 42.9 us
  Pallas kernels  41.4 us (96%)
  local copies, waits for them, and re-layouts  0.84 us (2%)
  between operations  0.66 us (2%)
    pallas_call x1, Pallas kernels, body(): pl.pallas_call(kernel, out_shape=jax.ShapeDtypeStruct((1, 5, DEPTH, WIDTH...  41.4 us

profile of v5, /device:TPU:1, one launch (start us, length us, event | category | flops | bytes accessed | tf_op | source)
XLA Modules:
  0.0 42.9 jit_solution(3171906582262651250)
XLA Ops:
  0.7 41.4 %shard_map.64 = f32[1,5,2,128,128]{4,3,2,1,0:T(8,128)S(1)} custom-call(f32[1,2,128,128]{3,2,1,0:T(8,128)} %start_hbm.1, f32[1,5,2,128,128]{4,3,2,1,0:T(8,128)} %force_hbm.1, f32[2,128,128]{2,1,0:T(8,128)} %first_hbm.1, f32[1]{0:T(128)S(6)} %copy.8.step_ref, f32[128,128]{1,0:T(8,128)} %constant.4.clone.sin_hbm, f32[128,128]{1,0:T(8,128)} %constant.5.clone.lamxy_hbm), custom_call_target="tpu_custom_call" | custom-call | tf_op jit(solution)/shard_map/pallas_call | solution.py:554
  42.1 0.8 %copy.9 = f32[1,5,2,128,128]{4,3,2,1,0:T(8,128)} copy(f32[1,5,2,128,128]{4,3,2,1,0:T(8,128)S(1)} %shard_map.64) | data formatting | bytes 1310720

commit v6 on v5

--- a/solution.py
+++ b/solution.py
@@ -26,7 +26,7 @@
 RING_ORDER = (4, 3, 5, 2, 6, 1, 7)
 GROUP_ORDER = (2, 1, 3)
 
-GUESS, FIRST, PSTEP, STEPS, GAINS, SHIFT = range(6)
+FIRST, PSTEP, STEPS, GAINS, NEXT, SHIFT, GUESS = range(7)
 FIELDS, SCAN, TOTALS, BACK, OUT = (8 + n * CHUNKS for n in range(5))
 PHASES = 8 + 5 * CHUNKS
 
@@ -145,7 +145,7 @@
 
 def kernel(
     start_hbm, force_hbm, first_hbm, step_ref, sin_hbm, lamxy_hbm, out_ref,
-    f_raw, g_raw, i_raw, sin_ref, lamxy, sin_hi, sin_lo, hat, gin, qin, firsts, ghat, shifted, guess,
+    f_raw, g_raw, i_raw, sin_ref, lamxy, sin_hi, sin_lo, hat, gin, qin, firsts, early, ghat, shifted, guess,
     earlier, qhat, lam, tab, alpha, pair_steps, step_tile, all_steps, gains, gain_all, fb, scan_in,
     totals, partial, back, cd, starts, yout, outr, measure, load_sem, send_sem, recv_sem, local_sem,
 ):
@@ -179,14 +179,14 @@
 
     sent = {}
 
-    def describe(src, dst, phase, target):
+    def describe(src, dst, leaving, phase, target):
         return pltpu.make_async_remote_copy(
-            src_ref=src, dst_ref=dst, send_sem=send_sem.at[phase], recv_sem=recv_sem.at[phase],
+            src_ref=src, dst_ref=dst, send_sem=send_sem.at[leaving], recv_sem=recv_sem.at[phase],
             device_id=target, device_id_type=MESH,
         )
 
     def send(src, dst, phase, target):
-        describe(src, dst, phase, target).start()
+        describe(src, dst, 0, phase, target).start()
         sent[phase] = sent.get(phase, 0) + math.prod(src.shape)
 
     def settle(sem, count):
@@ -204,9 +204,9 @@
     loads = [
         pltpu.make_async_copy(start_hbm.at[0], g_raw, load_sem.at[0]),
         pltpu.make_async_copy(sin_hbm, sin_ref, load_sem.at[1]),
+        pltpu.make_async_copy(first_hbm, i_raw, load_sem.at[4]),
         pltpu.make_async_copy(force_hbm.at[0], f_raw, load_sem.at[2]),
         pltpu.make_async_copy(lamxy_hbm.at[pl.ds(pl.multiple_of(own * COLS, COLS), COLS)], lamxy, load_sem.at[3]),
-        pltpu.make_async_copy(first_hbm, i_raw, load_sem.at[4]),
     ]
     for load in loads:
         load.start()
@@ -218,27 +218,38 @@
 
     for d in RING_ORDER:
         greet(along_ring(d)[1])
+    for d in range(SPACES):
+        greet((lax.rem(pair + pairs - 1, pairs) * 2 + 1, lax.rem(sp + d, SPACES)))
+    greet(following)
+    greet(preceding)
     for d in GROUP_ORDER:
         greet(across(d))
     for d in OWNER_ORDER:
         greet(owner(d)[1])
-    greet(following)
-    greet(preceding)
-
-    for load in loads[:2]:
+
+    for load in loads[:3]:
         load.wait()
     step = step_ref[0]
     pair_steps[half] = jnp.full((SUB, WIDTH), step, jnp.float32)
     sin_hi[...], sin_lo[...] = halves(sin_ref[...])
 
-    def transform(f, planes):
+    def transform(first, planes):
+        count = len(planes)
         wide = product(matrix(), halves(jnp.concatenate(planes, axis=1)))
-        tall = jnp.concatenate([wide[:, z * WIDTH : (z + 1) * WIDTH] for z in range(DEPTH)], axis=0)
-        hat[f] = product(halves(tall), matrix()).reshape(DEPTH, WIDTH, WIDTH)
-
-    transform(4, [g_raw[z] for z in range(DEPTH)])
-    loads[2].wait()
-    pl.semaphore_wait(barrier, OWNERS + RING + GROUPS - 1)
+        tall = jnp.concatenate([wide[:, z * WIDTH : (z + 1) * WIDTH] for z in range(count)], axis=0)
+        tall = product(halves(tall), matrix()).reshape(count // DEPTH, DEPTH, WIDTH, WIDTH)
+        hat[pl.ds(first, count // DEPTH)] = tall
+
+    transform(4, [g_raw[z] for z in range(DEPTH)] + [i_raw[z] for z in range(DEPTH)])
+    loads[3].wait()
+
+    def transform_fields(some):
+        transform(some[0], [
+            step * mixed(QUAD[m], [f_raw[j, z] for j in range(5)]) for m in some for z in range(DEPTH)
+        ])
+
+    transform_fields((0,))
+    pl.semaphore_wait(barrier, OWNERS + RING + GROUPS - 1 + OWNERS * half)
 
     mine = pl.ds(pl.multiple_of(own * COLS, COLS), COLS)
     here = pl.ds(sp * DEPTH, DEPTH)
@@ -254,18 +265,51 @@
         row = lax.broadcasted_iota(jnp.int32, (SUB, WIDTH), 0)
         return jnp.where(row < SPLIT, upper, lower)
 
+    next_pair = lax.rem(pair + 1, pairs)
+
+    @pl.when(half == 1)
+    def _():
+        for d in OWNER_ORDER + (0,):
+            other = lax.rem(own + d, OWNERS)
+            describe(
+                hat.at[4, :, slab(other, 0, SUB), :], early.at[here], 1, NEXT,
+                (next_pair * 2 + other // SPACES, lax.rem(other, SPACES)),
+            ).start()
+
     send(pair_steps.at[half], pair_steps.at[half], PSTEP, partner)
-    for d in OWNER_ORDER:
-        other, target = owner(d)
-        send(hat.at[4, :, slab(other, 0, COLS), :], gin.at[half, here], GUESS, target)
-    gin[half, here] = hat[4, :, mine, :]
-    for m in range(4):
-        transform(m, [
-            step * mixed(QUAD[m], [f_raw[j, z] for j in range(5)]) for z in range(DEPTH)
-        ])
+    def send_guess(n):
         for d in OWNER_ORDER:
             other, target = owner(d)
-            send(hat.at[m, :, slab(other, 0, SPLIT), :], qin.at[0, m, here, part, :], FIELDS, target)
+            rows = pl.ds(n * SUB, SUB)
+            send(hat.at[4, :, slab(other, n * SUB, SUB), :], gin.at[half, here, rows, :], GUESS + n, target)
+
+    send_guess(0)
+    first_size = (SPACES - 1) * DEPTH * COLS * WIDTH
+
+    @pl.when(pair == 0)
+    def _():
+        for d in range(1, SPACES):
+            other = lax.rem(sp + d, SPACES)
+            describe(
+                hat.at[5, :, slab(half * SPACES + other, 0, COLS), :], firsts.at[here], 2, FIRST, (tm, other)
+            ).start()
+        firsts[here] = hat[5, :, mine, :]
+
+    transform_fields((1, 2, 3))
+    gin[half, here] = hat[4, :, mine, :]
+
+    def send_fields(h):
+        for d in OWNER_ORDER:
+            other, target = owner(d)
+            send(
+                hat.at[pl.ds(0, 4), :, slab(other, h * SPLIT, SPLIT), :], qin.at[h, :, here, part, :],
+                FIELDS + h, target,
+            )
+
+    send_fields(0)
+    send_guess(1)
+    for h in range(1, CHUNKS):
+        send_fields(h)
     kept = [
         pltpu.make_async_copy(
             hat.at[pl.ds(0, 4), :, slab(own, h * SPLIT, SPLIT), :], qin.at[h, :, here, part, :], local_sem.at[h]
@@ -275,27 +319,7 @@
     for copy in kept:
         copy.start()
 
-    for load in loads[3:]:
-        load.wait()
-    first_size = (SPACES - 1) * DEPTH * COLS * WIDTH
-
-    @pl.when(pair == 0)
-    def _():
-        transform(5, [i_raw[z] for z in range(DEPTH)])
-        for d in range(1, SPACES):
-            other = lax.rem(sp + d, SPACES)
-            describe(
-                hat.at[5, :, slab(half * SPACES + other, 0, COLS), :], firsts.at[here], FIRST, (tm, other)
-            ).start()
-        firsts[here] = hat[5, :, mine, :]
-
-    def send_fields(h):
-        for d in OWNER_ORDER:
-            other, target = owner(d)
-            send(
-                hat.at[pl.ds(0, 4), :, slab(other, h * SPLIT, SPLIT), :], qin.at[h, :, here, part, :],
-                FIELDS + h, target,
-            )
+    loads[4].wait()
 
     z_matrix = sine(PLANES)
     z_eigen = eigen(PLANES)
@@ -305,12 +329,25 @@
         for k in range(PLANES):
             lam[h, k] = both + float(z_eigen[k])
 
+    def take_guess(n):
+        arrived(GUESS + n)
+        for s in (1, 0):
+            planes = along_z([gin[s, z, pl.ds(n * SUB, SUB), :] for z in range(PLANES)], z_matrix)
+            for k in range(PLANES):
+                ghat[s, n, k] = planes[k]
+            if s == 1 and n == 1:
+                send(ghat.at[1, n], shifted.at[n], SHIFT, following)
+        for h in (2 * n, 2 * n + 1):
+            for k in range(PLANES):
+                upper, lower = ghat[0, n, k], ghat[1, n, k]
+                guess[h, k] = pick(upper, swap(lower)) if h % 2 == 0 else pick(swap(upper), lower)
+
+    take_guess(0)
     arrived(PSTEP)
     step_tile[...] = pick(pair_steps[0], pair_steps[1])
     for d in RING_ORDER:
         send(step_tile, all_steps.at[slot], STEPS, along_ring(d)[1])
     all_steps[slot] = step_tile[...]
-
     def table(i, carry):
         two = pl.ds(i * 2, 2)
         for h in range(CHUNKS):
@@ -329,28 +366,12 @@
         return carry
 
     lax.fori_loop(0, PLANES // 2, table, 0)
-    send_fields(1)
-
-    arrived(GUESS)
-    for s in (1, 0):
-        for n in range(COLS // SUB):
-            planes = along_z([gin[s, z, pl.ds(n * SUB, SUB), :] for z in range(PLANES)], z_matrix)
-            for k in range(PLANES):
-                ghat[s, n, k] = planes[k]
-            if s == 1:
-                send(ghat.at[1, n], shifted.at[n], SHIFT + n, following)
-    for h in range(2, CHUNKS):
-        send_fields(h)
-    for h in range(CHUNKS):
-        for k in range(PLANES):
-            upper, lower = ghat[0, h // 2, k], ghat[1, h // 2, k]
-            guess[h, k] = pick(upper, swap(lower)) if h % 2 == 0 else pick(swap(upper), lower)
 
     opening = pick(jnp.where(pair == 0, 1.0, 0.0), 0.0)
 
     def pre(h):
         def step_pre(i, carry):
-            two = pl.ds(i * 2, 2)
+            two = pl.ds(i * 4, 4)
             mu = step_tile[...] * lam[h, two]
             before = earlier[h, two]
             f, v, left, b = sources([qhat[m, two] for m in range(4)], guess[h, two], before, mu)
@@ -371,9 +392,40 @@
             fb[h, two] = pick(swap(pair_f), pair_b)
             return carry
 
-        lax.fori_loop(0, PLANES // 2, step_pre, 0)
+        lax.fori_loop(0, PLANES // 4, step_pre, 0)
+
+    zero = jnp.zeros((SUB, WIDTH), jnp.float32)
+
+    def gain():
+        arrived(STEPS)
+
+        def pair_gain(i, carry):
+            out = []
+            for h in range(CHUNKS):
+                total_g, total_a = carry[h]
+                gains[i, 2, h] = total_g
+                gains[i, 3, h] = total_a
+                _, square, _, _, a = responses(all_steps[i] * lam[h, slot])
+                other = swap(square)
+                g = square * other
+                a = other * a
+                a = a + swap(a)
+                gains[i, 0, h] = g
+                gains[i, 1, h] = a
+                out.append((g * total_g, g * total_a + a * total_g))
+            return tuple(out)
+
+        ones = jnp.ones((SUB, WIDTH), jnp.float32)
+        ends = lax.fori_loop(0, RING, pair_gain, ((ones, zero),) * CHUNKS, unroll=4)
+        for h in range(CHUNKS):
+            gain_all[group, 0, h] = ends[h][0]
+            gain_all[group, 1, h] = ends[h][1]
+        for d in GROUP_ORDER:
+            send(gain_all.at[group], gain_all.at[group], GAINS, across(d))
 
     for h in range(CHUNKS):
+        if h == CHUNKS - 1:
+            gain()
         kept[h].wait()
         arrived(FIELDS + h)
         for m in range(4):
@@ -382,7 +434,13 @@
                 qhat[m, k] = planes[k]
         if h % 2 == 0:
             n = h // 2
-            arrived(SHIFT + n)
+            if n == 0:
+                settle(recv_sem.at[NEXT], PLANES * SUB * WIDTH)
+                planes = along_z([early[z] for z in range(PLANES)], z_matrix)
+                for k in range(PLANES):
+                    shifted[n, k] = planes[k]
+            else:
+                arrived(SHIFT)
 
             @pl.when(pair == 0)
             def _():
@@ -401,33 +459,8 @@
             other, target = along_ring(d)
             send(fb.at[h, other], scan_in.at[h, slot], SCAN + h, target)
         scan_in[h, slot] = fb[h, slot]
-
-    arrived(STEPS)
-
-    def pair_gain(i, carry):
-        out = []
-        for h in range(CHUNKS):
-            total_g, total_a = carry[h]
-            gains[i, 2, h] = total_g
-            gains[i, 3, h] = total_a
-            _, square, _, _, a = responses(all_steps[i] * lam[h, slot])
-            other = swap(square)
-            g = square * other
-            a = other * a
-            a = a + swap(a)
-            gains[i, 0, h] = g
-            gains[i, 1, h] = a
-            out.append((g * total_g, g * total_a + a * total_g))
-        return tuple(out)
-
-    ones = jnp.ones((SUB, WIDTH), jnp.float32)
-    zero = jnp.zeros((SUB, WIDTH), jnp.float32)
-    ends = lax.fori_loop(0, RING, pair_gain, ((ones, zero),) * CHUNKS)
-    for h in range(CHUNKS):
-        gain_all[group, 0, h] = ends[h][0]
-        gain_all[group, 1, h] = ends[h][1]
-    for d in GROUP_ORDER:
-        send(gain_all.at[group], gain_all.at[group], GAINS, across(d))
+        if h == 0:
+            take_guess(1)
 
     def advance(h):
         arrived(SCAN + h)
@@ -509,18 +542,14 @@
         copy.start()
         returned.append(copy)
 
-    advance(0)
-    advance(1)
-    advance(2)
+    for h in range(CHUNKS - 1):
+        advance(h)
     fold(0)
-    fold(1)
-    advance(3)
-    fold(2)
-    give(0)
-    fold(3)
-    give(1)
-    give(2)
-    give(3)
+    advance(CHUNKS - 1)
+    for h in range(1, CHUNKS):
+        fold(h)
+    for h in range(CHUNKS):
+        give(h)
 
     for h in range(CHUNKS):
         returned[h].wait()
@@ -531,12 +560,15 @@
         for z in range(DEPTH):
             out_ref[0, m, z] = wide[:, z * WIDTH : (z + 1) * WIDTH]
 
-    for phase, count in sent.items():
-        settle(send_sem.at[phase], count)
+    settle(send_sem.at[0], sum(sent.values()))
+
+    @pl.when(half == 1)
+    def _():
+        settle(send_sem.at[1], OWNERS * DEPTH * SUB * WIDTH)
 
     @pl.when(pair == 0)
     def _():
-        settle(send_sem.at[FIRST], first_size)
+        settle(send_sem.at[2], first_size)
 
 
 def body(initial, start_guess, forcing, step_size):
@@ -559,15 +591,15 @@
         scratch_shapes=[
             f32(5, DEPTH, WIDTH, WIDTH), f32(DEPTH, WIDTH, WIDTH), f32(DEPTH, WIDTH, WIDTH),
             f32(WIDTH, WIDTH), f32(COLS, WIDTH), bf16, bf16, f32(6, DEPTH, WIDTH, WIDTH),
-            f32(2, PLANES, COLS, WIDTH), f32(CHUNKS, 4, PLANES, *tile), f32(PLANES, COLS, WIDTH),
+            f32(2, PLANES, COLS, WIDTH), f32(CHUNKS, 4, PLANES, *tile), f32(PLANES, COLS, WIDTH), f32(PLANES, *tile),
             f32(2, COLS // SUB, PLANES, *tile), f32(COLS // SUB, PLANES, *tile), f32(CHUNKS, PLANES, *tile),
             f32(CHUNKS, PLANES, *tile), f32(4, PLANES, *tile), f32(CHUNKS, PLANES, *tile),
             f32(CHUNKS, 10, PLANES, *tile), f32(CHUNKS, 6, PLANES, *tile), f32(2, *tile), f32(*tile),
             f32(RING, *tile), f32(RING, 4, CHUNKS, *tile), f32(GROUPS, 2, CHUNKS, *tile),
             f32(CHUNKS, RING, *tile), f32(CHUNKS, RING, *tile), f32(CHUNKS, GROUPS, *tile),
             f32(CHUNKS, RING, 2, *tile), f32(CHUNKS, RING, *tile), f32(CHUNKS, RING, *tile),
-            f32(2, PLANES, *tile), f32(CHUNKS, 5, PLANES, *tile), f32(5, DEPTH, WIDTH, WIDTH), f32(80, *tile),
-            dma(5), dma(PHASES), dma(PHASES), dma(2 * CHUNKS),
+            f32(2, PLANES, *tile), f32(CHUNKS, 5, PLANES, *tile), f32(5, DEPTH, WIDTH, WIDTH), f32(480, *tile),
+            dma(5), dma(3), dma(PHASES), dma(2 * CHUNKS),
         ],
         compiler_params=pltpu.CompilerParams(
             collective_id=0, has_side_effects=True, vmem_limit_bytes=16 * 1024 * 1024

time: 43 us -> 40.7 us (0.947)
  Pallas kernels: 41.4 us -> 39.1 us
    pallas_call x1, Pallas kernels: 41.4 us -> 39.1 us  [body(): pl.pallas_call(kernel, out_shape=jax.ShapeDtypeStruct((1, 5, DEPTH, WIDTH...]
where the time goes in v6:
time: 40.7 us; the launch traced here: 40.6 us
  Pallas kernels  39.1 us (96%)
  local copies, waits for them, and re-layouts  0.84 us (2%)
  between operations  0.66 us (2%)
    pallas_call x1, Pallas kernels, body(): pl.pallas_call(kernel, out_shape=jax.ShapeDtypeStruct((1, 5, DEPTH, WIDTH...  39.1 us
    unnamed x1, local copies, waits for them, and re-layouts  0.84 us

profile of v6, /device:TPU:1, one launch (start us, length us, event | category | flops | bytes accessed | tf_op | source)
XLA Modules:
  0.0 40.6 jit_solution(3814659685351488588)
XLA Ops:
  0.7 39.1 %shard_map.64 = f32[1,5,2,128,128]{4,3,2,1,0:T(8,128)S(1)} custom-call(f32[1,2,128,128]{3,2,1,0:T(8,128)} %start_hbm.1, f32[1,5,2,128,128]{4,3,2,1,0:T(8,128)} %force_hbm.1, f32[2,128,128]{2,1,0:T(8,128)} %first_hbm.1, f32[1]{0:T(128)S(6)} %copy.8.step_ref, f32[128,128]{1,0:T(8,128)} %constant.4.clone.sin_hbm, f32[128,128]{1,0:T(8,128)} %constant.5.clone.lamxy_hbm), custom_call_target="tpu_custom_call" | custom-call | tf_op jit(solution)/shard_map/pallas_call | solution.py:586
  39.7 0.8 %copy.9 = f32[1,5,2,128,128]{4,3,2,1,0:T(8,128)} copy(f32[1,5,2,128,128]{4,3,2,1,0:T(8,128)S(1)} %shard_map.64) | data formatting | bytes 1310720

commit v7 on v6

--- a/solution.py
+++ b/solution.py
@@ -145,7 +145,7 @@
 
 def kernel(
     start_hbm, force_hbm, first_hbm, step_ref, sin_hbm, lamxy_hbm, out_ref,
-    f_raw, g_raw, i_raw, sin_ref, lamxy, sin_hi, sin_lo, hat, gin, qin, firsts, early, ghat, shifted, guess,
+    f_raw, g_raw, i_raw, sin_ref, lamxy, sin_left, sin_right, hat, gin, qin, firsts, early, ghat, shifted, guess,
     earlier, qhat, lam, tab, alpha, pair_steps, step_tile, all_steps, gains, gain_all, fb, scan_in,
     totals, partial, back, cd, starts, yout, outr, measure, load_sem, send_sem, recv_sem, local_sem,
 ):
@@ -159,12 +159,13 @@
         hi = x.astype(jnp.bfloat16)
         return hi, (x - hi.astype(jnp.float32)).astype(jnp.bfloat16)
 
-    def product(a, b):
-        dot = functools.partial(jnp.dot, preferred_element_type=jnp.float32)
-        return dot(a[0], b[0]) + (dot(a[0], b[1]) + dot(a[1], b[0]))
-
-    def matrix():
-        return sin_hi[...], sin_lo[...]
+    def from_left(x):
+        hi, lo = halves(x)
+        return jnp.dot(sin_left[...], jnp.concatenate([hi, lo, hi], axis=0), preferred_element_type=jnp.float32)
+
+    def from_right(x):
+        hi, lo = halves(x)
+        return jnp.dot(jnp.concatenate([hi, hi, lo], axis=1), sin_right[...], preferred_element_type=jnp.float32)
 
     def owner(d):
         other = lax.rem(own + d, OWNERS)
@@ -231,13 +232,15 @@
         load.wait()
     step = step_ref[0]
     pair_steps[half] = jnp.full((SUB, WIDTH), step, jnp.float32)
-    sin_hi[...], sin_lo[...] = halves(sin_ref[...])
+    hi, lo = halves(sin_ref[...])
+    sin_left[...] = jnp.concatenate([hi, hi, lo], axis=1)
+    sin_right[...] = jnp.concatenate([hi, lo, hi], axis=0)
 
     def transform(first, planes):
         count = len(planes)
-        wide = product(matrix(), halves(jnp.concatenate(planes, axis=1)))
+        wide = from_left(jnp.concatenate(planes, axis=1))
         tall = jnp.concatenate([wide[:, z * WIDTH : (z + 1) * WIDTH] for z in range(count)], axis=0)
-        tall = product(halves(tall), matrix()).reshape(count // DEPTH, DEPTH, WIDTH, WIDTH)
+        tall = from_right(tall).reshape(count // DEPTH, DEPTH, WIDTH, WIDTH)
         hat[pl.ds(first, count // DEPTH)] = tall
 
     transform(4, [g_raw[z] for z in range(DEPTH)] + [i_raw[z] for z in range(DEPTH)])
@@ -527,7 +530,7 @@
                         alpha[h, n, k] + (tab[h, 2 * n, k] * starts[0, k] + tab[h, 2 * n + 1, k] * starts[1, k])
                     )
             rows += along_z(planes, z_matrix)
-        rows = product(halves(jnp.concatenate(rows, axis=0)), matrix())
+        rows = from_right(jnp.concatenate(rows, axis=0))
         yout[h] = rows.reshape(5, PLANES, SUB, WIDTH)
         for d in OWNER_ORDER:
             other, target = owner(d)
@@ -556,7 +559,7 @@
         arrived(OUT + h)
     for m in range(5):
         wide = jnp.concatenate([outr[m, z] for z in range(DEPTH)], axis=1)
-        wide = product(matrix(), halves(wide))
+        wide = from_left(wide)
         for z in range(DEPTH):
             out_ref[0, m, z] = wide[:, z * WIDTH : (z + 1) * WIDTH]
 
@@ -578,7 +581,6 @@
     f32 = lambda *shape: pltpu.VMEM(shape, jnp.float32)
     dma = lambda *shape: pltpu.SemaphoreType.DMA(shape)
     tile = (SUB, WIDTH)
-    bf16 = pltpu.VMEM((WIDTH, WIDTH), jnp.bfloat16)
     start_guess, forcing, initial, table, lamxy = (
         pltpu.with_memory_space_constraint(x, pltpu.HBM)
         for x in (start_guess, forcing, initial, table, lamxy)
@@ -590,7 +592,7 @@
         out_specs=pl.BlockSpec(memory_space=pltpu.VMEM),
         scratch_shapes=[
             f32(5, DEPTH, WIDTH, WIDTH), f32(DEPTH, WIDTH, WIDTH), f32(DEPTH, WIDTH, WIDTH),
-            f32(WIDTH, WIDTH), f32(COLS, WIDTH), bf16, bf16, f32(6, DEPTH, WIDTH, WIDTH),
+            f32(WIDTH, WIDTH), f32(COLS, WIDTH), pltpu.VMEM((WIDTH, 3 * WIDTH), jnp.bfloat16), pltpu.VMEM((3 * WIDTH, WIDTH), jnp.bfloat16), f32(6, DEPTH, WIDTH, WIDTH),
             f32(2, PLANES, COLS, WIDTH), f32(CHUNKS, 4, PLANES, *tile), f32(PLANES, COLS, WIDTH), f32(PLANES, *tile),
             f32(2, COLS // SUB, PLANES, *tile), f32(COLS // SUB, PLANES, *tile), f32(CHUNKS, PLANES, *tile),
             f32(CHUNKS, PLANES, *tile), f32(4, PLANES, *tile), f32(CHUNKS, PLANES, *tile),

time: 40.7 us -> 40.5 us (level)
  no operation moved by 1% of the time
where the time goes in v7:
time: 40.5 us; the launch traced here: 40.4 us
  Pallas kernels  38.9 us (96%)
  local copies, waits for them, and re-layouts  0.84 us (2%)
  between operations  0.66 us (2%)
    pallas_call x1, Pallas kernels, body(): pl.pallas_call(kernel, out_shape=jax.ShapeDtypeStruct((1, 5, DEPTH, WIDTH...  38.9 us
    unnamed x1, local copies, waits for them, and re-layouts  0.84 us

profile of v7, /device:TPU:1, one launch (start us, length us, event | category | flops | bytes accessed | tf_op | source)
XLA Modules:
  0.0 40.4 jit_solution(557442634776486169)
XLA Ops:
  0.7 38.9 %shard_map.64 = f32[1,5,2,128,128]{4,3,2,1,0:T(8,128)S(1)} custom-call(f32[1,2,128,128]{3,2,1,0:T(8,128)} %start_hbm.1, f32[1,5,2,128,128]{4,3,2,1,0:T(8,128)} %force_hbm.1, f32[2,128,128]{2,1,0:T(8,128)} %first_hbm.1, f32[1]{0:T(128)S(6)} %copy.8.step_ref, f32[128,128]{1,0:T(8,128)} %constant.4.clone.sin_hbm, f32[128,128]{1,0:T(8,128)} %constant.5.clone.lamxy_hbm), custom_call_target="tpu_custom_call" | custom-call | tf_op jit(solution)/shard_map/pallas_call | solution.py:588
  39.6 0.8 %copy.9 = f32[1,5,2,128,128]{4,3,2,1,0:T(8,128)} copy(f32[1,5,2,128,128]{4,3,2,1,0:T(8,128)S(1)} %shard_map.64) | data formatting | bytes 1310720

commit v8 on v7

--- a/solution.py
+++ b/solution.py
@@ -287,6 +287,7 @@
             send(hat.at[4, :, slab(other, n * SUB, SUB), :], gin.at[half, here, rows, :], GUESS + n, target)
 
     send_guess(0)
+    send_guess(1)
     first_size = (SPACES - 1) * DEPTH * COLS * WIDTH
 
     @pl.when(pair == 0)
@@ -310,7 +311,6 @@
             )
 
     send_fields(0)
-    send_guess(1)
     for h in range(1, CHUNKS):
         send_fields(h)
     kept = [
@@ -370,11 +370,12 @@
 
     lax.fori_loop(0, PLANES // 2, table, 0)
 
+    take_guess(1)
     opening = pick(jnp.where(pair == 0, 1.0, 0.0), 0.0)
 
     def pre(h):
         def step_pre(i, carry):
-            two = pl.ds(i * 4, 4)
+            two = pl.ds(i * 8, 8)
             mu = step_tile[...] * lam[h, two]
             before = earlier[h, two]
             f, v, left, b = sources([qhat[m, two] for m in range(4)], guess[h, two], before, mu)
@@ -395,7 +396,7 @@
             fb[h, two] = pick(swap(pair_f), pair_b)
             return carry
 
-        lax.fori_loop(0, PLANES // 4, step_pre, 0)
+        lax.fori_loop(0, 1, step_pre, 0)
 
     zero = jnp.zeros((SUB, WIDTH), jnp.float32)
 
@@ -419,7 +420,7 @@
             return tuple(out)
 
         ones = jnp.ones((SUB, WIDTH), jnp.float32)
-        ends = lax.fori_loop(0, RING, pair_gain, ((ones, zero),) * CHUNKS, unroll=4)
+        ends = lax.fori_loop(0, RING, pair_gain, ((ones, zero),) * CHUNKS, unroll=8)
         for h in range(CHUNKS):
             gain_all[group, 0, h] = ends[h][0]
             gain_all[group, 1, h] = ends[h][1]
@@ -462,8 +463,6 @@
             other, target = along_ring(d)
             send(fb.at[h, other], scan_in.at[h, slot], SCAN + h, target)
         scan_in[h, slot] = fb[h, slot]
-        if h == 0:
-            take_guess(1)
 
     def advance(h):
         arrived(SCAN + h)

time: 40.5 us -> 40.1 us (level)
    pallas_call x1, Pallas kernels: 38.9 us -> 38.5 us  [body(): pl.pallas_call(kernel, out_shape=jax.ShapeDtypeStruct((1, 5, DEPTH, WIDTH...]
where the time goes in v8:
time: 40.1 us; the launch traced here: 40 us
  Pallas kernels  38.5 us (96%)
  local copies, waits for them, and re-layouts  0.84 us (2%)
  between operations  0.66 us (2%)
    pallas_call x1, Pallas kernels, body(): pl.pallas_call(kernel, out_shape=jax.ShapeDtypeStruct((1, 5, DEPTH, WIDTH...  38.5 us
    unnamed x1, local copies, waits for them, and re-layouts  0.84 us

profile of v8, /device:TPU:1, one launch (start us, length us, event | category | flops | bytes accessed | tf_op | source)
XLA Modules:
  0.0 40.0 jit_solution(8064335404142123831)
XLA Ops:
  0.7 38.5 %shard_map.64 = f32[1,5,2,128,128]{4,3,2,1,0:T(8,128)S(1)} custom-call(f32[1,2,128,128]{3,2,1,0:T(8,128)} %start_hbm.1, f32[1,5,2,128,128]{4,3,2,1,0:T(8,128)} %force_hbm.1, f32[2,128,128]{2,1,0:T(8,128)} %first_hbm.1, f32[1]{0:T(128)S(6)} %copy.8.step_ref, f32[128,128]{1,0:T(8,128)} %constant.4.clone.sin_hbm, f32[128,128]{1,0:T(8,128)} %constant.5.clone.lamxy_hbm), custom_call_target="tpu_custom_call" | custom-call | tf_op jit(solution)/shard_map/pallas_call | solution.py:587
  39.1 0.8 %copy.9 = f32[1,5,2,128,128]{4,3,2,1,0:T(8,128)} copy(f32[1,5,2,128,128]{4,3,2,1,0:T(8,128)S(1)} %shard_map.64) | data formatting | bytes 1310720
